TPU v7x, 32 devices: a 4x4x1 block of a 4x4x8 slice. The times are simulated.
32 devices in a mesh: data: 1 (over z), store: 4 (over y), model: 8 (over x, core).
Axes of the slice: x: 4, y: 4, z: 1, core: 2. Of those that a mesh axis runs over, the one named last changes fastest.
The devices are a block of a 4x4x8 slice.
Arguments:
- queries: bfloat16 [256, 2048], P('data')
- w_head: bfloat16 [2048, 32000], P(None, 'model')
- store_keys: bfloat16 [262144, 2048], P(('store', 'model'))
- store_tok: int32 [262144], P(('store', 'model'))
- temperature: float32 [], replicated
- mix_weight: float32 [], replicated
Outputs:
- output: float32 [256, 32000], P(('data', 'store'), 'model')
All inputs are finite; a program needn't handle non-finite values.
Results may differ from a plain program's by a relative error of at most 0.001.
Values are sent between devices in bfloat16 or wider.
A program may use at most 768 MiB of HBM per device.

v0:
```python
import jax
import jax.numpy as jnp
from jax import lax
from jax.sharding import PartitionSpec as P


def solution(mesh):
    store_devs = mesh.shape["store"]
    model_devs = mesh.shape["model"]
    group_axes = ("store", "model")

    def local_step(queries, w_head, store_keys, store_tok, value_a11, mix_weight):
        vocab_loc = w_head.shape[1]
        rows_loc = queries.shape[0] // store_devs
        key_dots = lax.dot_general(store_keys, queries, (((1,), (1,)), ((), ())), preferred_element_type=jnp.float32)
        key_norms = jnp.sum(jnp.square(store_keys.astype(jnp.float32)), axis=1)
        scores = (2.0 * key_dots - key_norms[:, None]) / value_a11
        row_top = lax.pmax(jnp.max(scores, axis=0), group_axes)
        weights = jnp.exp(scores - row_top)
        row_total = lax.psum(jnp.sum(weights, axis=0), group_axes)
        histogram = jax.ops.segment_sum(weights, store_tok, num_segments=vocab_loc * model_devs)
        histogram = lax.psum_scatter(histogram, "model", scatter_dimension=0, tiled=True)
        histogram = lax.psum_scatter(histogram, "store", scatter_dimension=1, tiled=True)
        row_start = lax.axis_index("store") * rows_loc
        my_rows = lax.dynamic_slice_in_dim(queries, row_start, rows_loc, axis=0)
        my_total = lax.dynamic_slice_in_dim(row_total, row_start, rows_loc)
        logits = lax.dot_general(w_head, my_rows, (((0,), (1,)), ((), ())), preferred_element_type=jnp.float32)
        lm_top = lax.pmax(jnp.max(logits, axis=0), "model")
        lm_exp = jnp.exp(logits - lm_top)
        lm_total = lax.psum(jnp.sum(lm_exp, axis=0), "model")
        mixed = mix_weight * (histogram / my_total) + (1.0 - mix_weight) * (lm_exp / lm_total)
        return jnp.log(mixed).T

    return jax.shard_map(local_step, mesh=mesh, in_specs=(P("data", None), P(None, "model"), P(group_axes, None), P(group_axes), P(), P()), out_specs=P(("data", "store"), "model"), check_vma=False)
```

profile of v0, /device:TPU:97, one launch (start us, length us, event | category | flops | bytes accessed | tf_op | source)
XLA Modules:
  0.0 411.5 jit_solution(14994221840070341585)
XLA Ops:
  6.5 0.0 copy-start
  6.6 0.0 reduce-scatter.7.cloned.1.call-start
  6.6 11.4 %multiply_reduce_fusion = f32[8192]{0:T(1024)S(1)} fusion(bf16[8192,2048]{1,0:T(8,128)(2,1)} %param.8), kind=kLoop, calls=%fused_computation.1 | loop fusion | flops 50323456 | bytes 33587200 | tf_op jit(solution)/shard_map/reduce_sum | solution.py:16
  18.6 0.0 copy-done
  18.6 17.6 %fusion.12 = (f32[256]{0:T(256)S(1)}, f32[8192,256]{1,0:T(8,128)}) fusion(f32[]{:T(128)S(6)} %copy.11, f32[8192]{0:T(1024)S(1)} %multiply_reduce_fusion, bf16[8192,2048]{1,0:T(8,128)(2,1)} %param.8, bf16[256,2048]{1,0:T(8,128)(2,1)S(1)} %copy-done), kind=kOutput, calls=%fused_computation.18 | convolution fusion | flops 8598323200 | bytes 43025412 | tf_op jit(solution)/shard_map/dot_general | solution.py:15
  36.2 49.9 %pmax.14 = f32[256]{0:T(256)S(1)} all-reduce(f32[256]{0:T(256)S(1)} %get-tuple-element.5), channel_id=1, replica_groups=mesh['data'=1,'store'=4,'model'=8] {'store','model'}, use_global_device_ids=true, to_apply=%region_2.0 | all-reduce | flops 256 | bytes 2048 | tf_op jit(solution)/shard_map/pmax | solution.py:18
  86.1 58.7 %scatter_custom_fusion = f32[32000,256]{1,0:T(8,128)} fusion(s32[8192]{0:T(1024)} %param.9, f32[]{:T(128)} %constant.8.clone.1, f32[8192,256]{1,0:T(8,128)} %get-tuple-element.6, f32[256]{0:T(256)S(1)} %pmax.14), kind=kCustom, calls=%fused_computation.2 | custom fusion | flops 4194304 | bytes 41158144 | tf_op jit(solution)/shard_map/scatter-add | solution.py:21
  144.8 0.1 reduce-scatter.7.cloned.1.call-update
  144.9 0.1 reduce-scatter.5.cloned.1.call-start
  144.9 161.9 %reduce-scatter.7.cloned.1.call-done = f32[4000,256]{1,0:T(8,128)} async-done(((f32[32000,256]{1,0:T(8,128)}), f32[4000,256]{1,0:T(8,128)}) %reduce-scatter.7.cloned.1.call-update) | async-done | bytes 4096016
  306.8 5.5 %copy.10 = f32[4000,256]{0,1:T(8,128)} copy(f32[4000,256]{1,0:T(8,128)} %reduce-scatter.7.cloned.1.call-done) | data formatting | bytes 8192000
  312.3 0.1 reduce-scatter.5.cloned.1.call-update
  313.0 4.5 %fusion.4 = f32[256]{0:T(256)S(1)} fusion(f32[8192,256]{1,0:T(8,128)} %get-tuple-element.6, f32[256]{0:T(256)S(1)} %pmax.14), kind=kLoop, calls=%fused_computation.8 | loop fusion | flops 4194048 | bytes 8390656 | tf_op jit(solution)/shard_map/reduce_sum | solution.py:20
  317.6 47.4 %psum.14 = f32[256]{0:T(256)S(1)} all-reduce(f32[256]{0:T(256)S(1)} %fusion.4), channel_id=1, replica_groups=mesh['data'=1,'store'=4,'model'=8] {'store','model'}, use_global_device_ids=true, to_apply=%region_7.0 | all-reduce | flops 256 | bytes 2048 | tf_op jit(solution)/shard_map/psum | solution.py:20
  365.0 0.1 dynamic_slice.6
  365.0 10.8 %fusion.13 = (f32[64]{0:T(128)S(1)}, f32[64,4000]{1,0:T(8,128)S(1)}) fusion(bf16[2048,4000]{0,1:T(8,128)(2,1)} %param.7, bf16[256,2048]{1,0:T(8,128)(2,1)S(1)} %copy-done, s32[]{:T(128)S(6)} %select_n.4), kind=kOutput, calls=%fused_computation.19 | convolution fusion | flops 1048831936 | bytes 17670404 | tf_op jit(solution)/shard_map/dot_general | solution.py:27
  375.9 13.1 %pmax.15 = f32[64]{0:T(128)S(1)} all-reduce(f32[64]{0:T(128)S(1)} %get-tuple-element.7), channel_id=1, replica_groups=mesh['data'=1,'store'=4,'model'=8] {'model'}, use_global_device_ids=true, to_apply=%region_9.0 | all-reduce | flops 64 | bytes 512 | tf_op jit(solution)/shard_map/pmax | solution.py:28
  389.0 0.3 fusion.8
  389.3 12.7 %psum.15 = f32[64]{0:T(128)S(1)} all-reduce(f32[64]{0:T(128)S(1)} %fusion.8), channel_id=1, replica_groups=mesh['data'=1,'store'=4,'model'=8] {'model'}, use_global_device_ids=true, to_apply=%region_11.0 | all-reduce | flops 64 | bytes 512 | tf_op jit(solution)/shard_map/psum | solution.py:30
  402.0 0.0 reduce-scatter.5.cloned.1.call-done
  402.0 2.6 fusion.7
Async XLA Ops:
  6.5 12.1 %copy-start = (bf16[256,2048]{1,0:T(8,128)(2,1)S(1)}, bf16[256,2048]{1,0:T(8,128)(2,1)}, u32[]{:S(2)}) copy-start(bf16[256,2048]{1,0:T(8,128)(2,1)} %param.6) | copy-start | bytes 3145732
  6.6 300.3 %reduce-scatter.7.cloned.1.call-start = ((), (), s32[]{:S(2)}) async-start(), calls=%async_computation.3 | async-start | bytes 36864000
  144.9 257.1 %reduce-scatter.5.cloned.1.call-start = ((), (), s32[]{:S(2)}) async-start(), calls=%async_computation.2 | async-start | bytes 5242880 | tf_op jit(solution)/shard_map/reduce_scatter | solution.py:23
Sparse Core Ops, SparseCore 0:
  145.0 161.7 reduce-scatter.6
  312.5 45.2 reduce-scatter.4
where the time goes:
time: 412 us; the launch traced here: 411 us
  waiting for transfers between devices  162 us (39%)
  blocking collectives  123 us (30%)
  other arithmetic  77.6 us (19%)
  matrix products  28.4 us (7%)
  between operations  14.8 us (4%)
  local copies, waits for them, and re-layouts  5.58 us (1%)
    unnamed x3, waiting for transfers between devices  162 us
    scatter-add x1, other arithmetic, local_step(): jax.ops.segment_sum(weights, store_tok, num_segments=vocab_loc * model_devs)  58.7 us
    pmax x1, blocking collectives, local_step(): row_top = lax.pmax(jnp.max(scores, axis=0), group_axes)  49.9 us
    psum x1, blocking collectives, local_step(): row_total = lax.psum(jnp.sum(weights, axis=0), group_axes)  47.4 us
    dot_general x1, matrix products, local_step(): lax.dot_general(store_keys, queries, (((1,), (1,)), ((), ())), preferred_...  17.6 us
    pmax x1, blocking collectives, local_step(): lm_top = lax.pmax(jnp.max(logits, axis=0), 'model')  13.1 us
    psum x1, blocking collectives, local_step(): lm_total = lax.psum(jnp.sum(lm_exp, axis=0), 'model')  12.7 us
    reduce_sum x1, other arithmetic, local_step(): key_norms = jnp.sum(jnp.square(store_keys.astype(jnp.float32)), axis=1)  11.4 us
  transfers between devices with their start and end apart: 2, of which 1 were waited for; matrix products, arithmetic and copies ran while one was open for 4% of the time, Pallas kernels for 0%

commit v1 on v0

v1 whole, which is shorter than its diff:
```python
import functools

import jax
import jax.numpy as jnp
from jax import lax
from jax.experimental import pallas as pl
from jax.experimental.pallas import tpu as pltpu
from jax.sharding import PartitionSpec as P

F32 = jnp.float32
BF16 = jnp.bfloat16
LANES = 128
BATCH = 4
MESH_ID = pl.DeviceIdType.MESH


def _scores_kernel(n_blocks, shards, tok_ref, rtau_ref, q_ref, k_ref, h_ref, stat_ref, hist, vals, top, stage, sem):
    step = pl.program_id(0)
    n_x, n_core, n_row, pairs, _ = shards
    block = k_ref.shape[0]
    rows = q_ref.shape[0]
    keys = vals.shape[0] // 2
    vocab = hist.shape[0] // 2

    zero_rows = hist.shape[0] // n_blocks
    zero_step = 64 if zero_rows % 64 == 0 else 8
    zero_base = step * zero_rows

    def clear(i, _):
        at = pl.multiple_of(zero_base + i * zero_step, 8)
        hist[pl.ds(at, zero_step), :] = jnp.zeros((zero_step, LANES), F32)
        return 0

    lax.fori_loop(0, zero_rows // zero_step, clear, 0)

    @pl.when(step == 0)
    def _():
        top[...] = jnp.full(top.shape, -jnp.inf, F32)

    sub = min(256, block)
    for part in range(block // sub):
        key = k_ref[part * sub : (part + 1) * sub, :]
        dots = lax.dot_general(key, q_ref[...], (((1,), (1,)), ((), ())), preferred_element_type=F32)
        wide = key.astype(F32)
        norms = jnp.sum(wide * wide, axis=1, keepdims=True)
        score = (2.0 * dots - norms) * rtau_ref[0]
        top[...] = jnp.maximum(top[...], jnp.max(score.reshape(sub // 8, 8, rows), axis=0))
        base = 2 * (step * block + part * sub)
        for half in range(2):
            vals[pl.ds(base + half, sub, stride=2), :] = score[:, half * LANES : (half + 1) * LANES]

    @pl.when(step == n_blocks - 1)
    def _():
        best = jnp.max(top[...], axis=0, keepdims=True)
        pair = jnp.concatenate([best[:, :LANES], best[:, LANES:]], axis=0)
        best8 = jnp.concatenate([pair] * 4, axis=0)

        def weigh(i, total):
            at = pl.multiple_of(i * 64, 64)
            old = vals[pl.ds(at, 64), :].reshape(8, 8, LANES)
            new = jnp.exp(old - best8[None])
            vals[pl.ds(at, 64), :] = new.reshape(64, LANES)
            return total + jnp.sum(new, axis=0)

        sum8 = lax.fori_loop(0, 2 * keys // 64, weigh, jnp.zeros((8, LANES), F32))
        total = sum8[0:2] + sum8[2:4] + sum8[4:6] + sum8[6:8]
        zeros6 = jnp.zeros((6, LANES), F32)
        stat_ref[...] = jnp.concatenate([pair, zeros6, total, zeros6], axis=0)

        per_trip = 4 * BATCH

        def scatter(i, _):
            first = i * per_trip
            for b in range(per_trip // BATCH):
                toks = [tok_ref[first + b * BATCH + j] for j in range(BATCH)]
                spots = [pl.ds(pl.multiple_of(2 * t, 2), 2) for t in toks]
                olds = [hist[p, :] for p in spots]
                news = []
                for j in range(BATCH):
                    base = olds[j]
                    for k in range(j):
                        base = jnp.where(toks[j] == toks[k], news[k], base)
                    at = pl.multiple_of(2 * (first + b * BATCH + j), 2)
                    news.append(base + vals[pl.ds(at, 2), :])
                for j in range(BATCH):
                    hist[spots[j], :] = news[j]
            return 0

        lax.fori_loop(0, keys // per_trip, scatter, 0)

        low = lax.broadcasted_iota(jnp.int32, (16, LANES), 1) < LANES // 2
        vocab_loc = 2 * pairs
        copies = []
        for owner in range(n_x * n_core):
            slot = owner % 2
            if owner >= 2:
                copies[owner - 2].wait()

            def pack(i, _, owner=owner, slot=slot):
                p = pl.multiple_of(i * 16, 16)
                for half in range(2):
                    a = hist[pl.ds(2 * (owner * vocab_loc + p) + half, 16, stride=2), :]
                    b = hist[pl.ds(2 * (owner * vocab_loc + pairs + p) + half, 16, stride=2), :]
                    stage[slot, 2 * half, pl.ds(p, 16), :] = jnp.where(low, a, pltpu.roll(b, 64, axis=1)).astype(BF16)
                    stage[slot, 2 * half + 1, pl.ds(p, 16), :] = jnp.where(low, pltpu.roll(a, 64, axis=1), b).astype(BF16)
                return 0

            lax.fori_loop(0, pairs // 16, pack, 0)
            copy = pltpu.make_async_copy(stage.at[slot], h_ref.at[owner // n_core, owner % n_core], sem.at[slot])
            copy.start()
            copies.append(copy)
        copies[-2].wait()
        copies[-1].wait()


def _exchange_kernel(ring, quarters, stat_ref, h_ref, out_ref, sout_ref,
                     own, par, ring1, ring2, fs, st_recv, st_buf,
                     own_sem, p_send, p_recv, r1_send, r1_recv, r2_send, r2_recv, st_send, st_rsem):
    s = lax.axis_index("store")
    m = lax.axis_index("model")
    x = lax.div(m, 2)
    c = lax.rem(m, 2)
    partner = {"store": s, "model": 2 * x + 1 - c}

    def along_y(d):
        return {"store": lax.rem(s + d + ring, ring), "model": m}

    def along_x(d):
        return {"store": s, "model": 2 * lax.rem(x + d + ring, ring) + c}

    barrier = pltpu.get_barrier_semaphore()
    peers = [partner] + [along_y(d) for d in range(1, ring)] + [along_x(d) for d in range(1, ring)]
    for peer in peers:
        pl.semaphore_signal(barrier, inc=1, device_id=peer, device_id_type=MESH_ID)
    pl.semaphore_wait(barrier, len(peers))

    sends = []

    def remote(src, dst, send_sem, recv_sem, peer):
        copy = pltpu.make_async_remote_copy(src_ref=src, dst_ref=dst, send_sem=send_sem, recv_sem=recv_sem,
                                            device_id=peer, device_id_type=MESH_ID)
        copy.start()
        sends.append(copy)
        return copy

    first_stat = remote(stat_ref, st_recv.at[0], st_send.at[0], st_rsem.at[0], partner)

    def direction(st):
        return 1 if st % 2 == 0 else -1

    def block_of(st, k):
        here = s if st < 2 else x
        return lax.rem(here - direction(st) * (k + 1) + 2 * ring, ring)

    def sub_of(st, i):
        here = x if st < 2 else s
        return lax.rem(here - direction(st) * (i + 1) + 2 * ring, ring)

    own_copies, par_copies = {}, {}
    for k in range(ring):
        for st in range(4):
            start, size = quarters[st]
            blk = block_of(st, k)
            slot = st * ring + k

            def view(core):
                if st < 2:
                    return h_ref.at[:, core, blk, pl.ds(start, size), :]
                return h_ref.at[blk, core, :, pl.ds(start, size), :]

            par_copies[st, k] = remote(view(1 - c), par.at[slot, :, pl.ds(0, size), :], p_send.at[slot], p_recv.at[slot], partner)
            mine = pltpu.make_async_copy(view(c), own.at[slot, :, pl.ds(0, size), :], own_sem.at[slot])
            mine.start()
            own_copies[st, k] = mine

    row_id = lax.broadcasted_iota(jnp.int32, (8, LANES), 0)

    def merge(a, b, keep_lm):
        high = jnp.maximum(a[0], b[0])
        total = a[1] * jnp.exp(a[0] - high) + b[1] * jnp.exp(b[0] - high)
        if keep_lm:
            high = jnp.where(row_id == 2, a[0], high)
            total = jnp.where(row_id == 2, a[1], total)
        return high, total

    def load(ref):
        return ref[0:8, :], ref[8:16, :]

    mine = load(stat_ref)
    first_stat.wait_recv()
    theirs = load(st_recv.at[0])
    now = merge(mine, theirs, False)
    for phase, (along, keep_lm) in enumerate(((along_y, True), (along_x, False))):
        st_buf[phase, 0:8, :] = now[0]
        st_buf[phase, 8:16, :] = now[1]
        copies = []
        for d in range(1, ring):
            n = 1 + phase * (ring - 1) + d - 1
            copies.append(remote(st_buf.at[phase], st_recv.at[n], st_send.at[n], st_rsem.at[n], along(d)))
        for d in range(1, ring):
            n = 1 + phase * (ring - 1) + d - 1
            copies[d - 1].wait_recv()
            now = merge(now, load(st_recv.at[n]), keep_lm)
    sout_ref[0:8, :] = now[0]
    sout_ref[8:16, :] = now[1]

    low = lax.broadcasted_iota(jnp.int32, (8, LANES), 1) < LANES // 2
    for who, stat in enumerate((mine, theirs)):
        factor = jnp.exp(stat[0] - now[0])
        for half in range(2):
            row = jnp.broadcast_to(factor[half : half + 1, :], (8, LANES))
            turned = pltpu.roll(row, 64, axis=1)
            fs[who, 2 * half] = jnp.where(low, row, turned)
            fs[who, 2 * half + 1] = jnp.where(low, turned, row)

    ring1_copies, ring2_copies = {}, {}

    def process(st, k, i):
        start, size = quarters[st]
        slot = st * ring + k
        sub = sub_of(st, i)
        band = block_of(st, k) if st < 2 else sub
        if i == 0:
            own_copies[st, k].wait()
            par_copies[st, k].wait_recv()
        if k > 0:
            ring1_copies[st, k - 1, i].wait_recv()
        last = k == ring - 1
        if last and i > 0:
            ring2_copies[st, i - 1].wait_recv()
        f_own = jnp.concatenate([fs[0, band]] * 2, axis=0)
        f_par = jnp.concatenate([fs[1, band]] * 2, axis=0)

        def add(at, count):
            for u in range(count):
                here = pl.ds(pl.multiple_of(at + 16 * u, 16), 16)
                value = own[slot, sub, here, :].astype(F32) * f_own + par[slot, sub, here, :].astype(F32) * f_par
                if k > 0:
                    value = value + ring1[st, k - 1, i, here, :].astype(F32)
                if last and i > 0:
                    value = value + ring2[st, i - 1, here, :].astype(F32)
                if last and i == ring - 1:
                    out_ref[pl.ds(pl.multiple_of(start + at + 16 * u, 16), 16), :] = value
                else:
                    own[slot, sub, here, :] = value.astype(BF16)

        units = size // 16
        full = units // 4

        def body(t, _):
            add(t * 64, 4)
            return 0

        if full:
            lax.fori_loop(0, full, body, 0)
        if units % 4:
            add(full * 64, units % 4)
        d = direction(st)
        if not last:
            peer = along_y(d) if st < 2 else along_x(d)
            ring1_copies[st, k, i] = remote(own.at[slot, sub, pl.ds(0, size), :], ring1.at[st, k, i, pl.ds(0, size), :],
                                            r1_send.at[st, k, i], r1_recv.at[st, k, i], peer)
        elif i < ring - 1:
            peer = along_x(d) if st < 2 else along_y(d)
            ring2_copies[st, i] = remote(own.at[slot, sub, pl.ds(0, size), :], ring2.at[st, i, pl.ds(0, size), :],
                                         r2_send.at[st, i], r2_recv.at[st, i], peer)

    for k in range(ring):
        for i in range(ring):
            for st in range(4):
                process(st, k, i)
    for copy in sends:
        copy.wait_send()


def _quarters(pairs):
    units = pairs // 16
    each = -(-units // 4)
    out, at = [], 0
    for n in range(4):
        size = min(each, units - at)
        out.append((at * 16, size * 16))
        at += size
    return tuple(out)


def solution(mesh):
    store_devs = mesh.shape["store"]
    model_devs = mesh.shape["model"]
    group_axes = ("store", "model")
    cores = 2
    n_x = model_devs // cores
    ring = store_devs

    def local_step(queries, w_head, store_keys, store_tok, temperature, mix_weight):
        vocab_loc = w_head.shape[1]
        vocab = vocab_loc * model_devs
        rows, hidden = queries.shape
        rows_loc = rows // store_devs
        keys = store_keys.shape[0]
        pairs = vocab_loc // 2
        block = min(512, keys)
        n_blocks = keys // block
        shards = (n_x, cores, store_devs, pairs, LANES)
        any_space = pl.BlockSpec(memory_space=pl.ANY)

        packed, stats = pl.pallas_call(
            functools.partial(_scores_kernel, n_blocks, shards),
            grid=(n_blocks,),
            out_shape=(jax.ShapeDtypeStruct(shards, BF16), jax.ShapeDtypeStruct((16, LANES), F32)),
            in_specs=[
                pl.BlockSpec(memory_space=pltpu.SMEM),
                pl.BlockSpec(memory_space=pltpu.SMEM),
                pl.BlockSpec((rows, hidden), lambda i: (0, 0)),
                pl.BlockSpec((block, hidden), lambda i: (i, 0)),
            ],
            out_specs=(any_space, pl.BlockSpec((16, LANES), lambda i: (0, 0))),
            scratch_shapes=[
                pltpu.VMEM((2 * vocab, LANES), F32),
                pltpu.VMEM((2 * keys, LANES), F32),
                pltpu.VMEM((8, rows), F32),
                pltpu.VMEM((2, store_devs, pairs, LANES), BF16),
                pltpu.SemaphoreType.DMA((2,)),
            ],
            compiler_params=pltpu.CompilerParams(vmem_limit_bytes=62 * 1024 * 1024),
            name="local_histogram",
        )(store_tok, (1.0 / temperature).reshape(1), queries, store_keys)

        row_start = lax.axis_index("store") * rows_loc
        my_rows = lax.dynamic_slice_in_dim(queries, row_start, rows_loc, axis=0)
        logits = lax.dot_general(w_head, my_rows, (((0,), (1,)), ((), ())), preferred_element_type=F32)
        lm_top = jnp.max(logits, axis=0)
        lm_sum = jnp.sum(jnp.exp(logits - lm_top), axis=0)
        stats = stats.at[2, :rows_loc].set(lm_top).at[10, :rows_loc].set(lm_sum)

        quarters = _quarters(pairs)
        most = quarters[0][1]
        dma = pltpu.SemaphoreType.DMA
        histogram, totals = pl.pallas_call(
            functools.partial(_exchange_kernel, ring, quarters),
            out_shape=(jax.ShapeDtypeStruct((pairs, LANES), F32), jax.ShapeDtypeStruct((16, LANES), F32)),
            in_specs=[pl.BlockSpec(memory_space=pltpu.VMEM), any_space],
            out_specs=(pl.BlockSpec(memory_space=pltpu.VMEM), pl.BlockSpec(memory_space=pltpu.VMEM)),
            scratch_shapes=[
                pltpu.VMEM((4 * ring, ring, most, LANES), BF16),
                pltpu.VMEM((4 * ring, ring, most, LANES), BF16),
                pltpu.VMEM((4, ring - 1, ring, most, LANES), BF16),
                pltpu.VMEM((4, ring - 1, most, LANES), BF16),
                pltpu.VMEM((2, ring, 8, LANES), F32),
                pltpu.VMEM((2 * ring - 1, 16, LANES), F32),
                pltpu.VMEM((2, 16, LANES), F32),
                dma((4 * ring,)), dma((4 * ring,)), dma((4 * ring,)),
                dma((4, ring - 1, ring)), dma((4, ring - 1, ring)),
                dma((4, ring - 1)), dma((4, ring - 1)),
                dma((2 * ring - 1,)), dma((2 * ring - 1,)),
            ],
            compiler_params=pltpu.CompilerParams(collective_id=0, has_side_effects=True, vmem_limit_bytes=48 * 1024 * 1024),
            name="group_exchange",
        )(stats, packed)

        my_total = lax.dynamic_slice_in_dim(totals[8:10].reshape(2 * LANES), row_start, rows_loc)
        lm_max, lm_total = totals[2, :rows_loc], totals[10, :rows_loc]
        summed = jnp.concatenate([histogram[:, : LANES // 2], histogram[:, LANES // 2 :]], axis=0)
        mixed = mix_weight * (summed / my_total) + (1.0 - mix_weight) * (jnp.exp(logits - lm_max) / lm_total)
        return jnp.log(mixed).T

    return jax.shard_map(local_step, mesh=mesh, in_specs=(P("data", None), P(None, "model"), P(group_axes, None), P(group_axes), P(), P()), out_specs=P(("data", "store"), "model"), check_vma=False)
```

time: 412 us -> 249 us (0.60)
  Pallas kernels: 0 us -> 223 us
  waiting for transfers between devices: 162 us -> 0 us
  blocking collectives: 123 us -> 0 us
  other arithmetic: 77.6 us -> 3.93 us
  matrix products: 28.4 us -> 10.9 us
  between operations: 14.8 us -> 1.4 us
    pallas_call x0 -> x2, Pallas kernels: none -> 223 us  [the longest x1 161 us: local_step(): pl.pallas_call(functools.partial(_scores_kernel, n_blocks, shards), grid=...]
    unnamed x3 -> x0, waiting for transfers between devices: 162 us -> none
    pmax x2 -> x0, blocking collectives: 63 us -> none  [the longest x1 49.9 us: local_step(): row_top = lax.pmax(jnp.max(scores, axis=0), group_axes)]
    psum x2 -> x0, blocking collectives: 60.1 us -> none  [the longest x1 47.4 us: local_step(): row_total = lax.psum(jnp.sum(weights, axis=0), group_axes)]
    scatter-add x1 -> x0, other arithmetic: 58.7 us -> none  [local_step(): jax.ops.segment_sum(weights, store_tok, num_segments=vocab_loc * model_devs)]
    dot_general x1 -> x0, matrix products: 17.6 us -> none  [local_step(): lax.dot_general(store_keys, queries, (((1,), (1,)), ((), ())), preferred_...]
    reduce_sum x3 -> x1, other arithmetic: 16.3 us -> 0.33 us  [local_step(): lm_sum = jnp.sum(jnp.exp(logits - lm_top), axis=0)]
    unnamed x3 -> x2, local copies, waits for them, and re-layouts: 5.51 us -> 0.7 us
  transfers between devices with their start and end apart: 2 -> 0, of which waited for: 1 -> 0; matrix products, arithmetic and copies ran while one was open for 4% -> 0% of each run, Pallas kernels for 0% -> 0%
where the time goes in v1:
time: 249 us; the launch traced here: 247 us
  Pallas kernels  223 us (90%)
  matrix products  10.9 us (4%)
  local copies, waits for them, and re-layouts  8.74 us (4%)
  other arithmetic  3.93 us (2%)
    pallas_call x1, Pallas kernels, local_step(): pl.pallas_call(functools.partial(_scores_kernel, n_blocks, shards), grid=...  161 us
    pallas_call x1, Pallas kernels, local_step(): pl.pallas_call(functools.partial(_exchange_kernel, ring, quarters), out_s...  61.5 us
    dot_general x1, matrix products, local_step(): lax.dot_general(w_head, my_rows, (((0,), (1,)), ((), ())), preferred_elem...  10.9 us

profile of v1, /device:TPU:97, one launch (start us, length us, event | category | flops | bytes accessed | tf_op | source)
XLA Modules:
  0.0 247.5 jit_solution(10952435855620125752)
XLA Ops:
  0.0 10.9 %fusion.8 = (f32[64]{0:T(128)S(1)}, f32[64,4000]{1,0:T(8,128)S(1)}) fusion(bf16[2048,4000]{0,1:T(8,128)(2,1)} %param.11, bf16[256,2048]{1,0:T(8,128)(2,1)} %q_ref.1, s32[]{:T(128)S(6)} %select_n.4), kind=kOutput, calls=%fused_computation.13 | convolution fusion | flops 1048831936 | bytes 17670404 | tf_op jit(solution)/shard_map/dot_general | solution.py:331
  10.9 0.3 exponential_reduce_fusion
  11.9 161.0 %local_histogram.1 = (bf16[4,2,4,2000,128]{4,3,2,1,0:T(8,128)(2,1)}, f32[16,128]{1,0:T(8,128)}) custom-call(s32[8192]{0:T(1024)} %tok_ref.1, f32[1]{0:T(128)} %bitcast.rtau_ref, bf16[256,2048]{1,0:T(8,128)(2,1)} %q_ref.1, bf16[8192,2048]{1,0:T(8,128)(2,1)} %k_ref.1), custom_call_target="tpu_custom_call" | custom-call | tf_op jit(solution)/shard_map/local_histogram/pallas_call | solution.py:307
  172.9 1.3 scatter.6
  174.3 1.3 scatter.9.stat_ref
  175.6 0.0 copy-start
  175.6 0.7 copy-done
  176.2 61.5 %group_exchange.1 = (f32[2000,128]{1,0:T(8,128)S(1)}, f32[16,128]{1,0:T(8,128)S(1)}) custom-call(f32[16,128]{1,0:T(8,128)S(1)} %copy-done, bf16[4,2,4,2000,128]{4,3,2,1,0:T(8,128)(2,1)} %get-tuple-element.34.h_ref), custom_call_target="tpu_custom_call" | custom-call | tf_op jit(solution)/shard_map/group_exchange/pallas_call | solution.py:339
  237.8 0.1 dynamic_slice.7
  237.9 1.6 fusion.7
  239.5 0.6 copy.9
  240.8 3.6 %fusion.3 = f32[64,4000]{0,1:T(8,128)} fusion(f32[2000,64]{1,0:T(8,128)} %get-tuple-element.38, f32[2000,64]{1,0:T(8,128)} %get-tuple-element.37, f32[64,4000]{0,1:T(8,128)S(1)} %copy.9, f32[]{:T(128)S(6)} %sub.25, f32[64]{0:T(128)S(1)} %get-tuple-element.40, f32[64]{0:T(128)S(1)} %get-tuple-element.39, f32[64]{0:T(128)S(1)} %dynamic_slice.7, f32[]{:T(128)S(6)} %copy.15), kind=kLoop, calls=%fused_computation.4 | loop fusion | flops 1792000 | bytes 3072776 | tf_op jit(solution)/shard_map/transpose | solution.py:365
  244.4 3.1 %copy.11 = f32[64,4000]{1,0:T(8,128)} copy(f32[64,4000]{0,1:T(8,128)} %fusion.3) | data formatting | bytes 2048000 | tf_op jit(solution)/shard_map/transpose | solution.py:365
  (2 shorter events, 0.0 us)
Async XLA Ops:
  175.6 0.7 copy-start

commit v2 on v1

v2 whole, which is shorter than its diff:
```python
import functools

import jax
import jax.numpy as jnp
from jax import lax
from jax.experimental import pallas as pl
from jax.experimental.pallas import tpu as pltpu
from jax.sharding import PartitionSpec as P

F32 = jnp.float32
BF16 = jnp.bfloat16
LANES = 128
BATCH = 32
GROUP = 16
PACK_TILES = 16
MESH_ID = pl.DeviceIdType.MESH


def _scores_kernel(n_blocks, owners, vocab_loc, tok_ref, rtau_ref, tok2_ref, q_ref, k_ref, h_ref, stat_ref, hist, vals, top, stage, flag_v, flag_s, sem, flag_sem):
    step = pl.program_id(0)
    n_core = h_ref.shape[1]
    first_half = h_ref.shape[3]
    block = k_ref.shape[0]
    rows = q_ref.shape[0]
    keys = vals.shape[0] // 2
    filled = 2 * vocab_loc * owners
    batch, n_batches = tok2_ref.shape

    zero_rows = filled // n_blocks
    hist[pl.ds(pl.multiple_of(step * zero_rows, 8), zero_rows), :] = jnp.zeros((zero_rows, LANES), F32)

    @pl.when(step == 0)
    def _():
        top[...] = jnp.full(top.shape, -jnp.inf, F32)
        rest = hist.shape[0] - filled
        hist[filled:, :] = jnp.zeros((rest, LANES), F32)
        toks = tok2_ref[...]
        same = jnp.zeros(toks.shape, jnp.int32)
        for d in range(1, batch // 2 + 1):
            same = jnp.maximum(same, jnp.where(toks == pltpu.roll(toks, d, axis=0), 1, 0))
        flag_v[...] = jnp.max(same, axis=0, keepdims=True)
        copy = pltpu.make_async_copy(flag_v, flag_s, flag_sem)
        copy.start()
        copy.wait()

    sub = min(256, block)
    for part in range(block // sub):
        key = k_ref[part * sub : (part + 1) * sub, :]
        dots = lax.dot_general(key, q_ref[...], (((1,), (1,)), ((), ())), preferred_element_type=F32)
        wide = key.astype(F32)
        norms = jnp.sum(wide * wide, axis=1, keepdims=True)
        score = (2.0 * dots - norms) * rtau_ref[0]
        top[...] = jnp.maximum(top[...], jnp.max(score.reshape(sub // 8, 8, rows), axis=0))
        base = 2 * (step * block + part * sub)
        for half in range(2):
            vals[pl.ds(base + half, sub, stride=2), :] = score[:, half * LANES : (half + 1) * LANES]

    @pl.when(step == n_blocks - 1)
    def _():
        best = jnp.max(top[...], axis=0, keepdims=True)
        pair = jnp.concatenate([best[:, :LANES], best[:, LANES:]], axis=0)
        best8 = jnp.concatenate([pair] * 4, axis=0)

        def weigh(i, total):
            at = pl.multiple_of(i * 128, 128)
            old = vals[pl.ds(at, 128), :].reshape(16, 8, LANES)
            new = jnp.exp(old - best8[None])
            vals[pl.ds(at, 128), :] = new.reshape(128, LANES)
            return total + jnp.sum(new, axis=0)

        sum8 = lax.fori_loop(0, 2 * keys // 128, weigh, jnp.zeros((8, LANES), F32))
        total = sum8[0:2] + sum8[2:4] + sum8[4:6] + sum8[6:8]
        zeros6 = jnp.zeros((6, LANES), F32)
        stat_ref[...] = jnp.concatenate([pair, zeros6, total, zeros6], axis=0)

        def value(u, i):
            return vals[pl.ds(pl.multiple_of(2 * (u * n_batches + i), 2), 2), :]

        def spots(i, members):
            out = []
            for u in members:
                word = tok_ref[u * n_batches + i]
                for at in (word & 0xFFFF, lax.shift_right_logical(word, 16)):
                    out.append(pl.ds(pl.multiple_of(at, 2), 2))
            return out, [v for u in members for v in (u, u + batch // 2)]

        def scatter(i, _):
            def distinct():
                for first in range(0, batch // 2, GROUP // 2):
                    at, who = spots(i, range(first, first + GROUP // 2))
                    news = [hist[p, :] + value(u, i) for p, u in zip(at, who)]
                    for p, new in zip(at, news):
                        hist[p, :] = new

            def repeated():
                for first in range(batch // 2):
                    for p, u in zip(*spots(i, [first])):
                        hist[p, :] = hist[p, :] + value(u, i)

            lax.cond(flag_s[0, i] > 0, repeated, distinct)
            return 0

        lax.fori_loop(0, n_batches, scatter, 0)

        low = lax.broadcasted_iota(jnp.int32, (16, LANES), 1) < LANES // 2
        tiles = PACK_TILES
        copies = []
        for owner in range(owners):
            slot = owner % 2
            if owner >= 2:
                copies[owner - 2].wait()

            def pack(i, _, owner=owner, slot=slot):
                for u in range(tiles):
                    p = pl.multiple_of(i * (16 * tiles) + u * 16, 16)
                    for half in range(2):
                        a = hist[pl.ds(2 * (owner * vocab_loc + p) + half, 16, stride=2), :]
                        b = hist[pl.ds(2 * (owner * vocab_loc + first_half + p) + half, 16, stride=2), :]
                        stage[slot, 2 * half, pl.ds(p, 16), :] = jnp.where(low, a, pltpu.roll(b, 64, axis=1)).astype(BF16)
                        stage[slot, 2 * half + 1, pl.ds(p, 16), :] = jnp.where(low, pltpu.roll(a, 64, axis=1), b).astype(BF16)
                return 0

            lax.fori_loop(0, first_half // (16 * tiles), pack, 0)
            copy = pltpu.make_async_copy(stage.at[slot], h_ref.at[owner // n_core, owner % n_core], sem.at[slot])
            copy.start()
            copies.append(copy)
        copies[-2].wait()
        copies[-1].wait()


def _exchange_kernel(ring, vocab_loc, lam_ref, stat_ref, q_ref, h_ref, w_ref, out_ref,
                     own, par, ring1, ring2, wbuf, logit, fin, qpad, lm_top, fs, st_recv, st_buf, lm_recv, lm_buf,
                     own_sem, p_send, p_recv, r1_send, r1_recv, r2_send, r2_recv, st_send, st_rsem, lm_send, lm_rsem, w_sem):
    s = lax.axis_index("store")
    m = lax.axis_index("model")
    x = lax.div(m, 2)
    c = lax.rem(m, 2)
    size = own.shape[2]
    first_half = 4 * size
    second_half = vocab_loc - first_half
    partner = {"store": s, "model": 2 * x + 1 - c}

    def along_y(d):
        return {"store": lax.rem(s + d + ring, ring), "model": m}

    def along_x(d):
        return {"store": s, "model": 2 * lax.rem(x + d + ring, ring) + c}

    barrier = pltpu.get_barrier_semaphore()
    peers = [partner] + [along_y(d) for d in range(1, ring)] + [along_x(d) for d in range(1, ring)]
    for peer in peers:
        pl.semaphore_signal(barrier, inc=1, device_id=peer, device_id_type=MESH_ID)
    pl.semaphore_wait(barrier, len(peers))

    sends = []

    def remote(src, dst, send_sem, recv_sem, peer):
        copy = pltpu.make_async_remote_copy(src_ref=src, dst_ref=dst, send_sem=send_sem, recv_sem=recv_sem,
                                            device_id=peer, device_id_type=MESH_ID)
        copy.start()
        sends.append(copy)
        return copy

    first_stat = remote(stat_ref, st_recv.at[0], st_send.at[0], st_rsem.at[0], partner)

    def direction(st):
        return 1 if st % 2 == 0 else -1

    def block_of(st, k):
        here = s if st < 2 else x
        return lax.rem(here - direction(st) * (k + 1) + 2 * ring, ring)

    def sub_of(st, i):
        here = x if st < 2 else s
        return lax.rem(here - direction(st) * (i + 1) + 2 * ring, ring)

    w_copies = {}

    def start_w(q):
        for half in range(2):
            count = size if half == 0 else min(size, second_half - q * size)
            if count <= 0:
                continue
            at = half * first_half + q * size
            copy = pltpu.make_async_copy(w_ref.at[pl.ds(at, count), :], wbuf.at[pl.ds(at, count), :], w_sem.at[half, q])
            copy.start()
            w_copies[q, half] = copy

    own_copies, par_copies = {}, {}
    for k in range(ring):
        for st in range(4):
            blk = block_of(st, k)
            slot = st * ring + k

            def view(core):
                if st < 2:
                    return h_ref.at[:, core, blk, pl.ds(st * size, size), :]
                return h_ref.at[blk, core, :, pl.ds(st * size, size), :]

            par_copies[st, k] = remote(view(1 - c), par.at[slot], p_send.at[slot], p_recv.at[slot], partner)
            mine = pltpu.make_async_copy(view(c), own.at[slot], own_sem.at[slot])
            mine.start()
            own_copies[st, k] = mine
        start_w(k)

    if second_half < first_half:
        wbuf[vocab_loc:, :] = jnp.zeros((2 * first_half - vocab_loc, wbuf.shape[1]), BF16)
    my_rows = q_ref[pl.ds(pl.multiple_of(s * 64, 64), 64), :]
    blank = jnp.zeros(my_rows.shape, BF16)
    qpad[0, 0:64, :] = my_rows
    qpad[0, 64:128, :] = blank
    qpad[1, 0:64, :] = blank
    qpad[1, 64:128, :] = my_rows

    def merge(a, b):
        high = jnp.maximum(a[0], b[0])
        return high, a[1] * jnp.exp(a[0] - high) + b[1] * jnp.exp(b[0] - high)

    def load(ref):
        return ref[0:8, :], ref[8:16, :]

    mine = load(stat_ref)
    first_stat.wait_recv()
    theirs = load(st_recv.at[0])
    now = merge(mine, theirs)
    for phase, along in enumerate((along_y, along_x)):
        st_buf[phase, 0:8, :] = now[0]
        st_buf[phase, 8:16, :] = now[1]
        copies = []
        for d in range(1, ring):
            n = 1 + phase * (ring - 1) + d - 1
            copies.append(remote(st_buf.at[phase], st_recv.at[n], st_send.at[n], st_rsem.at[n], along(d)))
        for d in range(1, ring):
            n = 1 + phase * (ring - 1) + d - 1
            copies[d - 1].wait_recv()
            now = merge(now, load(st_recv.at[n]))

    low = lax.broadcasted_iota(jnp.int32, (8, LANES), 1) < LANES // 2

    def spread(who, table):
        for half in range(2):
            row = jnp.broadcast_to(table[half : half + 1, :], (8, LANES))
            turned = pltpu.roll(row, 64, axis=1)
            fs[who, 2 * half] = jnp.where(low, row, turned)
            fs[who, 2 * half + 1] = jnp.where(low, turned, row)

    spread(0, jnp.exp(mine[0] - now[0]))
    spread(1, jnp.exp(theirs[0] - now[0]))
    spread(2, now[1])
    lam = lam_ref[0]

    ring1_copies, ring2_copies = {}, {}

    def process(st, k, i):
        slot = st * ring + k
        sub = sub_of(st, i)
        band = block_of(st, k) if st < 2 else sub
        if i == 0:
            own_copies[st, k].wait()
            par_copies[st, k].wait_recv()
        if k > 0:
            ring1_copies[st, k - 1, i].wait_recv()
        last = k == ring - 1
        if last and i > 0:
            ring2_copies[st, i - 1].wait_recv()
        f_own = jnp.concatenate([fs[0, band]] * 2, axis=0)
        f_par = jnp.concatenate([fs[1, band]] * 2, axis=0)
        unroll = 8 if size % 128 == 0 else 1

        def body(t, _):
            for u in range(unroll):
                here = pl.ds(pl.multiple_of(t * (16 * unroll) + 16 * u, 16), 16)
                value = own[slot, sub, here, :].astype(F32) * f_own + par[slot, sub, here, :].astype(F32) * f_par
                if k > 0:
                    value = value + ring1[st, k - 1, i, here, :].astype(F32)
                if last and i > 0:
                    value = value + ring2[st, i - 1, here, :].astype(F32)
                if last and i == ring - 1:
                    fin[here, :] = value
                else:
                    own[slot, sub, here, :] = value.astype(BF16)
            return 0

        lax.fori_loop(0, size // (16 * unroll), body, 0)
        d = direction(st)
        if not last:
            peer = along_y(d) if st < 2 else along_x(d)
            ring1_copies[st, k, i] = remote(own.at[slot, sub], ring1.at[st, k, i], r1_send.at[st, k, i], r1_recv.at[st, k, i], peer)
        elif i < ring - 1:
            peer = along_x(d) if st < 2 else along_y(d)
            ring2_copies[st, i] = remote(own.at[slot, sub], ring2.at[st, i], r2_send.at[st, i], r2_recv.at[st, i], peer)
        else:
            finish(st)

    def head(q):
        for half in range(2):
            if (q, half) in w_copies:
                w_copies[q, half].wait()
        contract = (((1,), (1,)), ((), ()))
        at = q * size
        part = lax.dot_general(wbuf[at : at + size, :], qpad[0], contract, preferred_element_type=F32)
        part = part + lax.dot_general(wbuf[first_half + at : first_half + at + size, :], qpad[1], contract, preferred_element_type=F32)
        if at + size > second_half:
            row = lax.broadcasted_iota(jnp.int32, (size, LANES), 0) + at
            lane = lax.broadcasted_iota(jnp.int32, (size, LANES), 1)
            part = jnp.where((row >= second_half) & (lane >= LANES // 2), -jnp.inf, part)
        logit[at : at + size, :] = part
        best = jnp.max(part.reshape(size // 8, 8, LANES), axis=0)
        lm_top[...] = best if q == 0 else jnp.maximum(lm_top[...], best)

    lm = {}

    def lm_local():
        best = jnp.max(lm_top[...], axis=0, keepdims=True)
        best = jnp.broadcast_to(best, (8, LANES))
        best = jnp.maximum(best, pltpu.roll(best, 64, axis=1))

        def body(t, total):
            here = pl.ds(pl.multiple_of(t * 64, 64), 64)
            new = jnp.exp(logit[here, :].reshape(8, 8, LANES) - best[None])
            logit[here, :] = new.reshape(64, LANES)
            return total + jnp.sum(new, axis=0)

        total = lax.fori_loop(0, first_half // 64, body, jnp.zeros((8, LANES), F32))
        total = jnp.broadcast_to(jnp.sum(total, axis=0, keepdims=True), (8, LANES))
        total = total + pltpu.roll(total, 64, axis=1)
        lm["mine"] = lm["now"] = (best, total)
        lm_publish(0, [partner])

    def lm_publish(phase, targets):
        lm_buf[phase, 0:8, :] = lm["now"][0]
        lm_buf[phase, 8:16, :] = lm["now"][1]
        lm["copies"] = [remote(lm_buf.at[phase], lm_recv.at[phase + n], lm_send.at[phase + n], lm_rsem.at[phase + n], peer)
                        for n, peer in enumerate(targets)]
        lm["slots"] = [phase + n for n in range(len(targets))]

    def lm_collect():
        for copy, n in zip(lm["copies"], lm["slots"]):
            copy.wait_recv()
            lm["now"] = merge(lm["now"], load(lm_recv.at[n]))

    def finish(st):
        scale = lam / fs[2, s]
        lm_scale = lm["scale"]
        wide = min(LANES, size)
        for b in range(size // wide):
            at = st * size + b * wide
            p_knn = fin[b * wide : (b + 1) * wide, :].reshape(wide // 8, 8, LANES) * scale[None]
            p_lm = logit[at : at + wide, :].reshape(wide // 8, 8, LANES) * lm_scale[None]
            mixed = jnp.log(p_knn + p_lm).reshape(wide, LANES).T
            out_ref[:, at : at + wide] = mixed[0:64, :]
            count = min(wide, second_half - at)
            if count > 0:
                out_ref[:, first_half + at : first_half + at + count] = mixed[64:128, :count]

    for k in range(ring):
        for i in range(ring):
            for st in range(4):
                process(st, k, i)
            if k == 0:
                head(i)
            if k == 1 and i == 0:
                lm_local()
            if k == 2 and i == 0:
                lm_collect()
                lm_publish(1, [along_x(d) for d in range(1, ring)])
            if k == 3 and i == 0:
                lm_collect()
                lm["scale"] = (1.0 - lam) * jnp.exp(lm["mine"][0] - lm["now"][0]) / lm["now"][1]
    for copy in sends:
        copy.wait_send()


def solution(mesh):
    store_devs = mesh.shape["store"]
    model_devs = mesh.shape["model"]
    group_axes = ("store", "model")
    cores = 2
    n_x = model_devs // cores
    ring = store_devs

    def local_step(queries, w_head, store_keys, store_tok, temperature, mix_weight):
        vocab_loc = w_head.shape[1]
        rows, hidden = queries.shape
        rows_loc = rows // store_devs
        keys = store_keys.shape[0]
        first_half = -(-vocab_loc // (2 * 4 * LANES)) * 4 * LANES
        size = first_half // 4
        block = min(512, keys)
        n_blocks = keys // block
        n_batches = keys // BATCH
        hist_rows = 2 * ((model_devs - 1) * vocab_loc + 2 * first_half)
        assert 2 * vocab_loc * model_devs <= 1 << 16
        words = 2 * store_tok[: keys // 2] | (2 * store_tok[keys // 2 :] << 16)
        any_space = pl.BlockSpec(memory_space=pl.ANY)
        smem = pl.BlockSpec(memory_space=pltpu.SMEM)
        vmem = pl.BlockSpec(memory_space=pltpu.VMEM)
        dma = pltpu.SemaphoreType.DMA

        packed, stats = pl.pallas_call(
            functools.partial(_scores_kernel, n_blocks, model_devs, vocab_loc),
            grid=(n_blocks,),
            out_shape=(jax.ShapeDtypeStruct((n_x, cores, store_devs, first_half, LANES), BF16), jax.ShapeDtypeStruct((16, LANES), F32)),
            in_specs=[
                smem,
                smem,
                pl.BlockSpec((BATCH, n_batches), lambda i: (0, 0)),
                pl.BlockSpec((rows, hidden), lambda i: (0, 0)),
                pl.BlockSpec((block, hidden), lambda i: (i, 0)),
            ],
            out_specs=(any_space, pl.BlockSpec((16, LANES), lambda i: (0, 0))),
            scratch_shapes=[
                pltpu.VMEM((hist_rows, LANES), F32),
                pltpu.VMEM((2 * keys, LANES), F32),
                pltpu.VMEM((8, rows), F32),
                pltpu.VMEM((2, store_devs, first_half, LANES), BF16),
                pltpu.VMEM((1, n_batches), jnp.int32),
                pltpu.SMEM((1, n_batches), jnp.int32),
                dma((2,)),
                dma,
            ],
            compiler_params=pltpu.CompilerParams(vmem_limit_bytes=62 * 1024 * 1024),
            name="local_histogram",
        )(words, (1.0 / temperature).reshape(1), store_tok.reshape(BATCH, n_batches), queries, store_keys)

        return pl.pallas_call(
            functools.partial(_exchange_kernel, ring, vocab_loc),
            out_shape=jax.ShapeDtypeStruct((rows_loc, vocab_loc), F32),
            in_specs=[smem, vmem, vmem, any_space, any_space],
            out_specs=vmem,
            scratch_shapes=[
                pltpu.VMEM((4 * ring, ring, size, LANES), BF16),
                pltpu.VMEM((4 * ring, ring, size, LANES), BF16),
                pltpu.VMEM((4, ring - 1, ring, size, LANES), BF16),
                pltpu.VMEM((4, ring - 1, size, LANES), BF16),
                pltpu.VMEM((2 * first_half, hidden), BF16),
                pltpu.VMEM((first_half, LANES), F32),
                pltpu.VMEM((size, LANES), F32),
                pltpu.VMEM((2, LANES, hidden), BF16),
                pltpu.VMEM((8, LANES), F32),
                pltpu.VMEM((3, ring, 8, LANES), F32),
                pltpu.VMEM((2 * ring - 1, 16, LANES), F32),
                pltpu.VMEM((2, 16, LANES), F32),
                pltpu.VMEM((ring, 16, LANES), F32),
                pltpu.VMEM((2, 16, LANES), F32),
                dma((4 * ring,)), dma((4 * ring,)), dma((4 * ring,)),
                dma((4, ring - 1, ring)), dma((4, ring - 1, ring)),
                dma((4, ring - 1)), dma((4, ring - 1)),
                dma((2 * ring - 1,)), dma((2 * ring - 1,)),
                dma((ring,)), dma((ring,)),
                dma((2, 4)),
            ],
            compiler_params=pltpu.CompilerParams(collective_id=0, has_side_effects=True, vmem_limit_bytes=62 * 1024 * 1024),
            name="group_exchange",
        )(mix_weight.reshape(1), stats, queries, packed, w_head.T)

    return jax.shard_map(local_step, mesh=mesh, in_specs=(P("data", None), P(None, "model"), P(group_axes, None), P(group_axes), P(), P()), out_specs=P(("data", "store"), "model"), check_vma=False)
```

time: 249 us -> 129 us (0.52)
  Pallas kernels: 223 us -> 121 us
  matrix products: 10.9 us -> 0 us
  local copies, waits for them, and re-layouts: 8.74 us -> 3.65 us
  other arithmetic: 3.93 us -> 1.34 us
    pallas_call x2, Pallas kernels: 223 us -> 121 us  [the longest x1 66.8 us: local_step(): pl.pallas_call(functools.partial(_exchange_kernel, ring, vocab_loc), out_...]
    dot_general x1 -> x0, matrix products: 10.9 us -> none  [local_step(): lax.dot_general(w_head, my_rows, (((0,), (1,)), ((), ())), preferred_elem...]
    transpose x1 -> x0, other arithmetic: 3.6 us -> none  [local_step(): return jnp.log(mixed).T]
    transpose x1 -> x0, local copies, waits for them, and re-layouts: 3.13 us -> none  [local_step(): return jnp.log(mixed).T]
    scatter x2 -> x0, local copies, waits for them, and re-layouts: 2.6 us -> none  [local_step(): stats = stats.at[2, :rows_loc].set(lm_top).at[10, :rows_loc].set(lm_sum)]
where the time goes in v2:
time: 129 us; the launch traced here: 127 us
  Pallas kernels  121 us (94%)
  local copies, waits for them, and re-layouts  3.65 us (3%)
  between operations  1.35 us (1%)
  other arithmetic  1.34 us (1%)
    pallas_call x1, Pallas kernels, local_step(): pl.pallas_call(functools.partial(_exchange_kernel, ring, vocab_loc), out_...  66.8 us
    pallas_call x1, Pallas kernels, local_step(): pl.pallas_call(functools.partial(_scores_kernel, n_blocks, model_devs, vo...  54.1 us

profile of v2, /device:TPU:97, one launch (start us, length us, event | category | flops | bytes accessed | tf_op | source)
XLA Modules:
  0.0 127.2 jit_solution(1193128769973132335)
XLA Ops:
  1.3 1.3 %shift-left_or_fusion.tok_ref = s32[4096]{0:T(1024)} fusion(s32[8192]{0:T(1024)} %param.9), kind=kLoop, calls=%fused_computation | loop fusion | flops 16384 | bytes 49152 | tf_op jit(solution)/shard_map/or | solution.py:394
  2.7 1.4 %reshape.11.tok2_ref = s32[32,256]{1,0:T(8,128)} reshape(s32[8192]{0:T(1024)} %param.9) | data formatting | bytes 65536 | tf_op jit(solution)/shard_map/reshape | solution.py:424
  4.1 54.1 %local_histogram.1 = (bf16[4,2,4,2048,128]{4,3,2,1,0:T(8,128)(2,1)}, f32[16,128]{1,0:T(8,128)}) custom-call(s32[4096]{0:T(1024)} %shift-left_or_fusion.tok_ref, f32[1]{0:T(128)} %bitcast.1.rtau_ref, s32[32,256]{1,0:T(8,128)} %reshape.11.tok2_ref, bf16[256,2048]{1,0:T(8,128)(2,1)} %q_ref.3, bf16[8192,2048]{1,0:T(8,128)(2,1)} %k_ref.1), custom_call_target="tpu_custom_call" | custom-call | tf_op jit(solution)/shard_map/local_histogram/pallas_call | solution.py:400
  58.1 66.8 %group_exchange.1 = f32[64,4000]{1,0:T(8,128)} custom-call(f32[1]{0:T(128)} %bitcast.3.lam_ref, f32[16,128]{1,0:T(8,128)} %get-tuple-element.7.stat_ref, bf16[256,2048]{1,0:T(8,128)(2,1)} %q_ref.3, bf16[4,2,4,2048,128]{4,3,2,1,0:T(8,128)(2,1)} %get-tuple-element.8.h_ref, bf16[4000,2048]{1,0:T(8,128)(2,1)} %bitcast.4), custom_call_target="tpu_custom_call" | custom-call | tf_op jit(solution)/shard_map/group_exchange/pallas_call | solution.py:426
  125.0 2.3 %copy.10 = f32[64,4000]{1,0:T(8,128)} copy(f32[64,4000]{1,0:T(8,128)} %group_exchange.1) | data formatting | bytes 2048000

commit v3 on v2

--- a/solution.py
+++ b/solution.py
@@ -14,6 +14,7 @@
 GROUP = 16
 PACK_TILES = 16
 MESH_ID = pl.DeviceIdType.MESH
+ORDER = ((0, 0), (0, 1), (0, 2), (1, 0), (0, 3), (1, 1), (2, 0), (1, 2), (2, 1), (3, 0), (1, 3), (2, 2), (3, 1), (2, 3), (3, 2), (3, 3))
 
 
 def _scores_kernel(n_blocks, owners, vocab_loc, tok_ref, rtau_ref, tok2_ref, q_ref, k_ref, h_ref, stat_ref, hist, vals, top, stage, flag_v, flag_s, sem, flag_sem):
@@ -187,21 +188,33 @@
             w_copies[q, half] = copy
 
     own_copies, par_copies = {}, {}
-    for k in range(ring):
+
+    def fetch(st, k, sub, sem):
+        blk = block_of(st, k)
+        slot = st * ring + k
+        rows = pl.ds(st * size, size)
+
+        def view(core):
+            if sub is None:
+                return h_ref.at[:, core, blk, rows, :] if st < 2 else h_ref.at[blk, core, :, rows, :]
+            return h_ref.at[sub, core, blk, rows, :] if st < 2 else h_ref.at[blk, core, sub, rows, :]
+
+        def into(ref):
+            return ref.at[slot] if sub is None else ref.at[slot, sub]
+
+        par_copies[st, sem] = remote(view(1 - c), into(par), p_send.at[st, sem], p_recv.at[st, sem], partner)
+        mine = pltpu.make_async_copy(view(c), into(own), own_sem.at[st, sem])
+        mine.start()
+        own_copies[st, sem] = mine
+
+    for i in range(ring):
         for st in range(4):
-            blk = block_of(st, k)
-            slot = st * ring + k
-
-            def view(core):
-                if st < 2:
-                    return h_ref.at[:, core, blk, pl.ds(st * size, size), :]
-                return h_ref.at[blk, core, :, pl.ds(st * size, size), :]
-
-            par_copies[st, k] = remote(view(1 - c), par.at[slot], p_send.at[slot], p_recv.at[slot], partner)
-            mine = pltpu.make_async_copy(view(c), own.at[slot], own_sem.at[slot])
-            mine.start()
-            own_copies[st, k] = mine
-        start_w(k)
+            fetch(st, 0, sub_of(st, i), i)
+    for k in range(1, ring):
+        start_w(k - 1)
+        for st in range(4):
+            fetch(st, k, None, ring + k - 1)
+    start_w(ring - 1)
 
     if second_half < first_half:
         wbuf[vocab_loc:, :] = jnp.zeros((2 * first_half - vocab_loc, wbuf.shape[1]), BF16)
@@ -219,22 +232,6 @@
     def load(ref):
         return ref[0:8, :], ref[8:16, :]
 
-    mine = load(stat_ref)
-    first_stat.wait_recv()
-    theirs = load(st_recv.at[0])
-    now = merge(mine, theirs)
-    for phase, along in enumerate((along_y, along_x)):
-        st_buf[phase, 0:8, :] = now[0]
-        st_buf[phase, 8:16, :] = now[1]
-        copies = []
-        for d in range(1, ring):
-            n = 1 + phase * (ring - 1) + d - 1
-            copies.append(remote(st_buf.at[phase], st_recv.at[n], st_send.at[n], st_rsem.at[n], along(d)))
-        for d in range(1, ring):
-            n = 1 + phase * (ring - 1) + d - 1
-            copies[d - 1].wait_recv()
-            now = merge(now, load(st_recv.at[n]))
-
     low = lax.broadcasted_iota(jnp.int32, (8, LANES), 1) < LANES // 2
 
     def spread(who, table):
@@ -244,9 +241,38 @@
             fs[who, 2 * half] = jnp.where(low, row, turned)
             fs[who, 2 * half + 1] = jnp.where(low, turned, row)
 
-    spread(0, jnp.exp(mine[0] - now[0]))
-    spread(1, jnp.exp(theirs[0] - now[0]))
-    spread(2, now[1])
+    mine = load(stat_ref)
+    first_stat.wait_recv()
+    theirs = load(st_recv.at[0])
+    knn = {"now": merge(mine, theirs)}
+    spread(0, jnp.exp(mine[0] - knn["now"][0]))
+    spread(1, jnp.exp(theirs[0] - knn["now"][0]))
+
+    def knn_publish(phase, targets):
+        st_buf[phase, 0:8, :] = knn["now"][0]
+        st_buf[phase, 8:16, :] = knn["now"][1]
+        knn["copies"] = []
+        for n, peer in targets:
+            knn["copies"].append((n, remote(st_buf.at[phase], st_recv.at[n], st_send.at[n], st_rsem.at[n], peer)))
+
+    def knn_collect():
+        for n, copy in knn["copies"]:
+            copy.wait_recv()
+            if n < 2 * ring - 1:
+                knn["now"] = merge(knn["now"], load(st_recv.at[n]))
+
+    side = 2 * ring - 1
+    knn_publish(0, [(d, along_y(d)) for d in range(1, ring)] + [(side, along_x(1)), (side + 1, along_x(-1))])
+
+    def knn_group():
+        knn_collect()
+        high = knn["now"][0]
+        spread(2, jnp.exp(mine[0] - high))
+        spread(3, jnp.exp(theirs[0] - high))
+        spread(4, knn["now"][1])
+        for st, n in enumerate((1, ring - 1, side, side + 1)):
+            spread(5 + st, jnp.exp(st_recv[n, 0:8, :] - high))
+
     lam = lam_ref[0]
 
     ring1_copies, ring2_copies = {}, {}
@@ -255,16 +281,18 @@
         slot = st * ring + k
         sub = sub_of(st, i)
         band = block_of(st, k) if st < 2 else sub
-        if i == 0:
-            own_copies[st, k].wait()
-            par_copies[st, k].wait_recv()
+        if k == 0 or i == 0:
+            sem = i if k == 0 else ring + k - 1
+            own_copies[st, sem].wait()
+            par_copies[st, sem].wait_recv()
         if k > 0:
             ring1_copies[st, k - 1, i].wait_recv()
         last = k == ring - 1
         if last and i > 0:
             ring2_copies[st, i - 1].wait_recv()
-        f_own = jnp.concatenate([fs[0, band]] * 2, axis=0)
-        f_par = jnp.concatenate([fs[1, band]] * 2, axis=0)
+        f_own = jnp.concatenate([fs[0 if k == 0 else 2, band]] * 2, axis=0)
+        f_par = jnp.concatenate([fs[1 if k == 0 else 3, band]] * 2, axis=0)
+        f_ring = jnp.concatenate([fs[5 + st, band]] * 2, axis=0) if k == 1 else None
         unroll = 8 if size % 128 == 0 else 1
 
         def body(t, _):
@@ -272,7 +300,8 @@
                 here = pl.ds(pl.multiple_of(t * (16 * unroll) + 16 * u, 16), 16)
                 value = own[slot, sub, here, :].astype(F32) * f_own + par[slot, sub, here, :].astype(F32) * f_par
                 if k > 0:
-                    value = value + ring1[st, k - 1, i, here, :].astype(F32)
+                    came = ring1[st, k - 1, i, here, :].astype(F32)
+                    value = value + (came * f_ring if k == 1 else came)
                 if last and i > 0:
                     value = value + ring2[st, i - 1, here, :].astype(F32)
                 if last and i == ring - 1:
@@ -340,7 +369,7 @@
             lm["now"] = merge(lm["now"], load(lm_recv.at[n]))
 
     def finish(st):
-        scale = lam / fs[2, s]
+        scale = lam / fs[4, s]
         lm_scale = lm["scale"]
         wide = min(LANES, size)
         for b in range(size // wide):
@@ -353,20 +382,24 @@
             if count > 0:
                 out_ref[:, first_half + at : first_half + at + count] = mixed[64:128, :count]
 
-    for k in range(ring):
-        for i in range(ring):
-            for st in range(4):
-                process(st, k, i)
-            if k == 0:
-                head(i)
-            if k == 1 and i == 0:
-                lm_local()
-            if k == 2 and i == 0:
-                lm_collect()
-                lm_publish(1, [along_x(d) for d in range(1, ring)])
-            if k == 3 and i == 0:
-                lm_collect()
-                lm["scale"] = (1.0 - lam) * jnp.exp(lm["mine"][0] - lm["now"][0]) / lm["now"][1]
+    for place, (k, i) in enumerate(ORDER):
+        for st in range(4):
+            process(st, k, i)
+        if place == 0:
+            knn_collect()
+            knn_publish(1, [(ring - 1 + d, along_x(d)) for d in range(1, ring)])
+        if place == 2:
+            knn_group()
+        if place in (3, 4, 6, 7):
+            head((3, 4, 6, 7).index(place))
+        if place == 8:
+            lm_local()
+        if place == 10:
+            lm_collect()
+            lm_publish(1, [along_x(d) for d in range(1, ring)])
+        if place == 12:
+            lm_collect()
+            lm["scale"] = (1.0 - lam) * jnp.exp(lm["mine"][0] - lm["now"][0]) / lm["now"][1]
     for copy in sends:
         copy.wait_send()
 
@@ -386,7 +419,7 @@
         keys = store_keys.shape[0]
         first_half = -(-vocab_loc // (2 * 4 * LANES)) * 4 * LANES
         size = first_half // 4
-        block = min(512, keys)
+        block = min(1024, keys)
         n_blocks = keys // block
         n_batches = keys // BATCH
         hist_rows = 2 * ((model_devs - 1) * vocab_loc + 2 * first_half)
@@ -438,19 +471,19 @@
                 pltpu.VMEM((size, LANES), F32),
                 pltpu.VMEM((2, LANES, hidden), BF16),
                 pltpu.VMEM((8, LANES), F32),
-                pltpu.VMEM((3, ring, 8, LANES), F32),
-                pltpu.VMEM((2 * ring - 1, 16, LANES), F32),
+                pltpu.VMEM((9, ring, 8, LANES), F32),
+                pltpu.VMEM((2 * ring + 1, 16, LANES), F32),
                 pltpu.VMEM((2, 16, LANES), F32),
                 pltpu.VMEM((ring, 16, LANES), F32),
                 pltpu.VMEM((2, 16, LANES), F32),
-                dma((4 * ring,)), dma((4 * ring,)), dma((4 * ring,)),
+                dma((4, 2 * ring - 1)), dma((4, 2 * ring - 1)), dma((4, 2 * ring - 1)),
                 dma((4, ring - 1, ring)), dma((4, ring - 1, ring)),
                 dma((4, ring - 1)), dma((4, ring - 1)),
-                dma((2 * ring - 1,)), dma((2 * ring - 1,)),
+                dma((2 * ring + 1,)), dma((2 * ring + 1,)),
                 dma((ring,)), dma((ring,)),
                 dma((2, 4)),
             ],
-            compiler_params=pltpu.CompilerParams(collective_id=0, has_side_effects=True, vmem_limit_bytes=62 * 1024 * 1024),
+            compiler_params=pltpu.CompilerParams(collective_id=0, has_side_effects=True, vmem_limit_bytes=52 * 1024 * 1024),
             name="group_exchange",
         )(mix_weight.reshape(1), stats, queries, packed, w_head.T)
 

time: 129 us -> 115 us (0.89)
  Pallas kernels: 121 us -> 109 us
    pallas_call x1, Pallas kernels: 66.8 us -> 58.9 us  [local_step(): pl.pallas_call(functools.partial(_exchange_kernel, ring, vocab_loc), out_...]
    pallas_call x1, Pallas kernels: 54.1 us -> 49.8 us  [local_step(): pl.pallas_call(functools.partial(_scores_kernel, n_blocks, model_devs, vo...]
where the time goes in v3:
time: 115 us; the launch traced here: 114 us
  Pallas kernels  109 us (95%)
  local copies, waits for them, and re-layouts  3.04 us (3%)
  between operations  1.36 us (1%)
  other arithmetic  1.34 us (1%)
    pallas_call x1, Pallas kernels, local_step(): pl.pallas_call(functools.partial(_exchange_kernel, ring, vocab_loc), out_...  58.9 us
    pallas_call x1, Pallas kernels, local_step(): pl.pallas_call(functools.partial(_scores_kernel, n_blocks, model_devs, vo...  49.8 us

profile of v3, /device:TPU:97, one launch (start us, length us, event | category | flops | bytes accessed | tf_op | source)
XLA Modules:
  0.0 114.4 jit_solution(56283231082640068)
XLA Ops:
  1.3 1.3 %shift-left_or_fusion.tok_ref = s32[4096]{0:T(1024)} fusion(s32[8192]{0:T(1024)} %param.9), kind=kLoop, calls=%fused_computation | loop fusion | flops 16384 | bytes 49152 | tf_op jit(solution)/shard_map/or | solution.py:427
  2.7 1.4 %reshape.11.tok2_ref = s32[32,256]{1,0:T(8,128)} reshape(s32[8192]{0:T(1024)} %param.9) | data formatting | bytes 65536 | tf_op jit(solution)/shard_map/reshape | solution.py:457
  4.1 49.8 %local_histogram.1 = (bf16[4,2,4,2048,128]{4,3,2,1,0:T(8,128)(2,1)}, f32[16,128]{1,0:T(8,128)}) custom-call(s32[4096]{0:T(1024)} %shift-left_or_fusion.tok_ref, f32[1]{0:T(128)} %bitcast.1.rtau_ref, s32[32,256]{1,0:T(8,128)} %reshape.11.tok2_ref, bf16[256,2048]{1,0:T(8,128)(2,1)} %q_ref.3, bf16[8192,2048]{1,0:T(8,128)(2,1)} %k_ref.1), custom_call_target="tpu_custom_call" | custom-call | tf_op jit(solution)/shard_map/local_histogram/pallas_call | solution.py:433
  53.8 0.0 copy-start
  53.8 0.7 copy-done
  54.5 58.9 %group_exchange.1 = f32[64,4000]{1,0:T(8,128)S(1)} custom-call(f32[1]{0:T(128)} %bitcast.3.lam_ref, f32[16,128]{1,0:T(8,128)S(1)} %copy-done, bf16[256,2048]{1,0:T(8,128)(2,1)} %q_ref.3, bf16[4,2,4,2048,128]{4,3,2,1,0:T(8,128)(2,1)} %get-tuple-element.8.h_ref, bf16[4000,2048]{1,0:T(8,128)(2,1)} %bitcast.4), custom_call_target="tpu_custom_call" | custom-call | tf_op jit(solution)/shard_map/group_exchange/pallas_call | solution.py:459
  113.4 1.0 copy.10
Async XLA Ops:
  53.8 0.7 copy-start

commit v4 on v3

--- a/solution.py
+++ b/solution.py
@@ -12,12 +12,12 @@
 LANES = 128
 BATCH = 32
 GROUP = 16
-PACK_TILES = 16
+PACK_TILES = 32
 MESH_ID = pl.DeviceIdType.MESH
 ORDER = ((0, 0), (0, 1), (0, 2), (1, 0), (0, 3), (1, 1), (2, 0), (1, 2), (2, 1), (3, 0), (1, 3), (2, 2), (3, 1), (2, 3), (3, 2), (3, 3))
 
 
-def _scores_kernel(n_blocks, owners, vocab_loc, tok_ref, rtau_ref, tok2_ref, q_ref, k_ref, h_ref, stat_ref, hist, vals, top, stage, flag_v, flag_s, sem, flag_sem):
+def _scores_kernel(n_blocks, owners, vocab_loc, tok_ref, rtau_ref, q_ref, k_ref, h_ref, stat_ref, hist, vals, top, stage, flag_v, flag_s, word_v, word_s, sem, token_sem):
     step = pl.program_id(0)
     n_core = h_ref.shape[1]
     first_half = h_ref.shape[3]
@@ -25,7 +25,9 @@
     rows = q_ref.shape[0]
     keys = vals.shape[0] // 2
     filled = 2 * vocab_loc * owners
-    batch, n_batches = tok2_ref.shape
+    batch, n_batches = BATCH, keys // BATCH
+
+    token_copies = [pltpu.make_async_copy(word_v, word_s, token_sem.at[0]), pltpu.make_async_copy(flag_v, flag_s, token_sem.at[1])]
 
     zero_rows = filled // n_blocks
     hist[pl.ds(pl.multiple_of(step * zero_rows, 8), zero_rows), :] = jnp.zeros((zero_rows, LANES), F32)
@@ -35,14 +37,16 @@
         top[...] = jnp.full(top.shape, -jnp.inf, F32)
         rest = hist.shape[0] - filled
         hist[filled:, :] = jnp.zeros((rest, LANES), F32)
-        toks = tok2_ref[...]
-        same = jnp.zeros(toks.shape, jnp.int32)
-        for d in range(1, batch // 2 + 1):
-            same = jnp.maximum(same, jnp.where(toks == pltpu.roll(toks, d, axis=0), 1, 0))
-        flag_v[...] = jnp.max(same, axis=0, keepdims=True)
-        copy = pltpu.make_async_copy(flag_v, flag_s, flag_sem)
-        copy.start()
-        copy.wait()
+        rows_t = [tok_ref[pl.ds(u * n_batches, n_batches)] for u in range(batch)]
+        same = jnp.zeros(rows_t[0].shape, jnp.int32)
+        for u in range(batch):
+            for v in range(u):
+                same = jnp.maximum(same, jnp.where(rows_t[u] == rows_t[v], 1, 0))
+        flag_v[0, :] = same
+        for u in range(batch // 2):
+            word_v[0, pl.ds(u * n_batches, n_batches)] = 2 * rows_t[u] | (2 * rows_t[u + batch // 2] << 16)
+        for copy in token_copies:
+            copy.start()
 
     sub = min(256, block)
     for part in range(block // sub):
@@ -60,48 +64,48 @@
     def _():
         best = jnp.max(top[...], axis=0, keepdims=True)
         pair = jnp.concatenate([best[:, :LANES], best[:, LANES:]], axis=0)
-        best8 = jnp.concatenate([pair] * 4, axis=0)
-
-        def weigh(i, total):
-            at = pl.multiple_of(i * 128, 128)
-            old = vals[pl.ds(at, 128), :].reshape(16, 8, LANES)
-            new = jnp.exp(old - best8[None])
-            vals[pl.ds(at, 128), :] = new.reshape(128, LANES)
-            return total + jnp.sum(new, axis=0)
-
-        sum8 = lax.fori_loop(0, 2 * keys // 128, weigh, jnp.zeros((8, LANES), F32))
-        total = sum8[0:2] + sum8[2:4] + sum8[4:6] + sum8[6:8]
-        zeros6 = jnp.zeros((6, LANES), F32)
-        stat_ref[...] = jnp.concatenate([pair, zeros6, total, zeros6], axis=0)
+        for copy in token_copies:
+            copy.wait()
 
         def value(u, i):
-            return vals[pl.ds(pl.multiple_of(2 * (u * n_batches + i), 2), 2), :]
+            return jnp.exp(vals[pl.ds(pl.multiple_of(2 * (u * n_batches + i), 2), 2), :] - pair)
 
         def spots(i, members):
             out = []
             for u in members:
-                word = tok_ref[u * n_batches + i]
+                word = word_s[0, u * n_batches + i]
                 for at in (word & 0xFFFF, lax.shift_right_logical(word, 16)):
                     out.append(pl.ds(pl.multiple_of(at, 2), 2))
             return out, [v for u in members for v in (u, u + batch // 2)]
 
-        def scatter(i, _):
+        def scatter(i, total):
             def distinct():
+                sums = []
                 for first in range(0, batch // 2, GROUP // 2):
                     at, who = spots(i, range(first, first + GROUP // 2))
-                    news = [hist[p, :] + value(u, i) for p, u in zip(at, who)]
-                    for p, new in zip(at, news):
-                        hist[p, :] = new
+                    olds = [hist[p, :] for p in at]
+                    adds = [value(u, i) for u in who]
+                    for p, old, add in zip(at, olds, adds):
+                        hist[p, :] = old + add
+                    sums += adds
+                while len(sums) > 1:
+                    sums = [a + b for a, b in zip(sums[::2], sums[1::2])]
+                return sums[0]
 
             def repeated():
+                some = jnp.zeros((2, LANES), F32)
                 for first in range(batch // 2):
                     for p, u in zip(*spots(i, [first])):
-                        hist[p, :] = hist[p, :] + value(u, i)
-
-            lax.cond(flag_s[0, i] > 0, repeated, distinct)
-            return 0
-
-        lax.fori_loop(0, n_batches, scatter, 0)
+                        add = value(u, i)
+                        hist[p, :] = hist[p, :] + add
+                        some = some + add
+                return some
+
+            return total + lax.cond(flag_s[0, i] > 0, repeated, distinct)
+
+        total = lax.fori_loop(0, n_batches, scatter, jnp.zeros((2, LANES), F32))
+        zeros6 = jnp.zeros((6, LANES), F32)
+        stat_ref[...] = jnp.concatenate([pair, zeros6, total, zeros6], axis=0)
 
         low = lax.broadcasted_iota(jnp.int32, (16, LANES), 1) < LANES // 2
         tiles = PACK_TILES
@@ -129,9 +133,9 @@
         copies[-1].wait()
 
 
-def _exchange_kernel(ring, vocab_loc, lam_ref, stat_ref, q_ref, h_ref, w_ref, out_ref,
-                     own, par, ring1, ring2, wbuf, logit, fin, qpad, lm_top, fs, st_recv, st_buf, lm_recv, lm_buf,
-                     own_sem, p_send, p_recv, r1_send, r1_recv, r2_send, r2_recv, st_send, st_rsem, lm_send, lm_rsem, w_sem):
+def _exchange_kernel(ring, vocab_loc, lam_ref, stat_hbm, q_ref, h_ref, w_ref, out_ref,
+                     own, par, ring1, ring2, wbuf, logit, fin, qpad, stat_ref, lm_top, fs, st_recv, st_buf, lm_recv, lm_buf,
+                     own_sem, p_send, p_recv, r1_send, r1_recv, r2_send, r2_recv, st_send, st_rsem, lm_send, lm_rsem, w_sem, in_sem):
     s = lax.axis_index("store")
     m = lax.axis_index("model")
     x = lax.div(m, 2)
@@ -147,12 +151,6 @@
     def along_x(d):
         return {"store": s, "model": 2 * lax.rem(x + d + ring, ring) + c}
 
-    barrier = pltpu.get_barrier_semaphore()
-    peers = [partner] + [along_y(d) for d in range(1, ring)] + [along_x(d) for d in range(1, ring)]
-    for peer in peers:
-        pl.semaphore_signal(barrier, inc=1, device_id=peer, device_id_type=MESH_ID)
-    pl.semaphore_wait(barrier, len(peers))
-
     sends = []
 
     def remote(src, dst, send_sem, recv_sem, peer):
@@ -161,8 +159,6 @@
         copy.start()
         sends.append(copy)
         return copy
-
-    first_stat = remote(stat_ref, st_recv.at[0], st_send.at[0], st_rsem.at[0], partner)
 
     def direction(st):
         return 1 if st % 2 == 0 else -1
@@ -189,7 +185,7 @@
 
     own_copies, par_copies = {}, {}
 
-    def fetch(st, k, sub, sem):
+    def fetch(st, k, sub, sem, mine):
         blk = block_of(st, k)
         slot = st * ring + k
         rows = pl.ds(st * size, size)
@@ -202,28 +198,46 @@
         def into(ref):
             return ref.at[slot] if sub is None else ref.at[slot, sub]
 
-        par_copies[st, sem] = remote(view(1 - c), into(par), p_send.at[st, sem], p_recv.at[st, sem], partner)
-        mine = pltpu.make_async_copy(view(c), into(own), own_sem.at[st, sem])
-        mine.start()
-        own_copies[st, sem] = mine
-
-    for i in range(ring):
-        for st in range(4):
-            fetch(st, 0, sub_of(st, i), i)
+        if mine:
+            own_copies[st, sem] = pltpu.make_async_copy(view(c), into(own), own_sem.at[st, sem])
+            own_copies[st, sem].start()
+        else:
+            par_copies[st, sem] = remote(view(1 - c), into(par), p_send.at[st, sem], p_recv.at[st, sem], partner)
+
+    def fetch_first(mine):
+        for i in range(ring):
+            for st in range(4):
+                fetch(st, 0, sub_of(st, i), i, mine)
+
+    stat_copy = pltpu.make_async_copy(stat_hbm, stat_ref, in_sem.at[0])
+    stat_copy.start()
+    fetch_first(True)
+    my_rows = q_ref.at[pl.ds(pl.multiple_of(s * 64, 64), 64), :]
+    q_copies = [pltpu.make_async_copy(my_rows, qpad.at[n, pl.ds(64 * n, 64), :], in_sem.at[1 + n]) for n in range(2)]
+    for copy in q_copies:
+        copy.start()
+
+    barrier = pltpu.get_barrier_semaphore()
+    peers = [partner] + [along_y(d) for d in range(1, ring)] + [along_x(d) for d in range(1, ring)]
+    for peer in peers:
+        pl.semaphore_signal(barrier, inc=1, device_id=peer, device_id_type=MESH_ID)
+    pl.semaphore_wait(barrier, len(peers))
+
+    stat_copy.wait()
+    first_stat = remote(stat_ref, st_recv.at[0], st_send.at[0], st_rsem.at[0], partner)
+    fetch_first(False)
     for k in range(1, ring):
         start_w(k - 1)
         for st in range(4):
-            fetch(st, k, None, ring + k - 1)
+            fetch(st, k, None, ring + k - 1, False)
+            fetch(st, k, None, ring + k - 1, True)
     start_w(ring - 1)
 
     if second_half < first_half:
         wbuf[vocab_loc:, :] = jnp.zeros((2 * first_half - vocab_loc, wbuf.shape[1]), BF16)
-    my_rows = q_ref[pl.ds(pl.multiple_of(s * 64, 64), 64), :]
-    blank = jnp.zeros(my_rows.shape, BF16)
-    qpad[0, 0:64, :] = my_rows
+    blank = jnp.zeros((64, qpad.shape[2]), BF16)
     qpad[0, 64:128, :] = blank
     qpad[1, 0:64, :] = blank
-    qpad[1, 64:128, :] = my_rows
 
     def merge(a, b):
         high = jnp.maximum(a[0], b[0])
@@ -322,6 +336,9 @@
             finish(st)
 
     def head(q):
+        if q == 0:
+            for copy in q_copies:
+                copy.wait()
         for half in range(2):
             if (q, half) in w_copies:
                 w_copies[q, half].wait()
@@ -424,10 +441,10 @@
         n_batches = keys // BATCH
         hist_rows = 2 * ((model_devs - 1) * vocab_loc + 2 * first_half)
         assert 2 * vocab_loc * model_devs <= 1 << 16
-        words = 2 * store_tok[: keys // 2] | (2 * store_tok[keys // 2 :] << 16)
         any_space = pl.BlockSpec(memory_space=pl.ANY)
         smem = pl.BlockSpec(memory_space=pltpu.SMEM)
         vmem = pl.BlockSpec(memory_space=pltpu.VMEM)
+        hbm = pl.BlockSpec(memory_space=pltpu.HBM)
         dma = pltpu.SemaphoreType.DMA
 
         packed, stats = pl.pallas_call(
@@ -435,9 +452,8 @@
             grid=(n_blocks,),
             out_shape=(jax.ShapeDtypeStruct((n_x, cores, store_devs, first_half, LANES), BF16), jax.ShapeDtypeStruct((16, LANES), F32)),
             in_specs=[
+                pl.BlockSpec((keys,), lambda i: (0,)),
                 smem,
-                smem,
-                pl.BlockSpec((BATCH, n_batches), lambda i: (0, 0)),
                 pl.BlockSpec((rows, hidden), lambda i: (0, 0)),
                 pl.BlockSpec((block, hidden), lambda i: (i, 0)),
             ],
@@ -449,17 +465,19 @@
                 pltpu.VMEM((2, store_devs, first_half, LANES), BF16),
                 pltpu.VMEM((1, n_batches), jnp.int32),
                 pltpu.SMEM((1, n_batches), jnp.int32),
+                pltpu.VMEM((1, keys // 2), jnp.int32),
+                pltpu.SMEM((1, keys // 2), jnp.int32),
                 dma((2,)),
-                dma,
+                dma((2,)),
             ],
             compiler_params=pltpu.CompilerParams(vmem_limit_bytes=62 * 1024 * 1024),
             name="local_histogram",
-        )(words, (1.0 / temperature).reshape(1), store_tok.reshape(BATCH, n_batches), queries, store_keys)
+        )(store_tok, (1.0 / temperature).reshape(1), queries, store_keys)
 
         return pl.pallas_call(
             functools.partial(_exchange_kernel, ring, vocab_loc),
             out_shape=jax.ShapeDtypeStruct((rows_loc, vocab_loc), F32),
-            in_specs=[smem, vmem, vmem, any_space, any_space],
+            in_specs=[smem, hbm, hbm, hbm, hbm],
             out_specs=vmem,
             scratch_shapes=[
                 pltpu.VMEM((4 * ring, ring, size, LANES), BF16),
@@ -470,6 +488,7 @@
                 pltpu.VMEM((first_half, LANES), F32),
                 pltpu.VMEM((size, LANES), F32),
                 pltpu.VMEM((2, LANES, hidden), BF16),
+                pltpu.VMEM((16, LANES), F32),
                 pltpu.VMEM((8, LANES), F32),
                 pltpu.VMEM((9, ring, 8, LANES), F32),
                 pltpu.VMEM((2 * ring + 1, 16, LANES), F32),
@@ -482,6 +501,7 @@
                 dma((2 * ring + 1,)), dma((2 * ring + 1,)),
                 dma((ring,)), dma((ring,)),
                 dma((2, 4)),
+                dma((3,)),
             ],
             compiler_params=pltpu.CompilerParams(collective_id=0, has_side_effects=True, vmem_limit_bytes=52 * 1024 * 1024),
             name="group_exchange",

time: 115 us -> 108 us (0.939)
  Pallas kernels: 109 us -> 104 us
  local copies, waits for them, and re-layouts: 3.04 us -> 1.66 us
  other arithmetic: 1.34 us -> 0 us
    pallas_call x1, Pallas kernels: 49.8 us -> 46.5 us  [local_step(): pl.pallas_call(functools.partial(_scores_kernel, n_blocks, model_devs, vo...]
    reshape x1 -> x0, local copies, waits for them, and re-layouts: 1.38 us -> none  [local_step(): store_tok.reshape(BATCH, n_batches)]
    or x1 -> x0, other arithmetic: 1.34 us -> none  [local_step(): words = 2 * store_tok[:keys // 2] | 2 * store_tok[keys // 2:] << 16]
where the time goes in v4:
time: 108 us; the launch traced here: 107 us
  Pallas kernels  104 us (96%)
  local copies, waits for them, and re-layouts  1.66 us (2%)
  between operations  1.36 us (1%)
    pallas_call x1, Pallas kernels, local_step(): pl.pallas_call(functools.partial(_exchange_kernel, ring, vocab_loc), out_...  57.8 us
    pallas_call x1, Pallas kernels, local_step(): pl.pallas_call(functools.partial(_scores_kernel, n_blocks, model_devs, vo...  46.5 us

profile of v4, /device:TPU:97, one launch (start us, length us, event | category | flops | bytes accessed | tf_op | source)
XLA Modules:
  0.0 107.3 jit_solution(12065423169849665439)
XLA Ops:
  1.3 46.5 %local_histogram.1 = (bf16[4,2,4,2048,128]{4,3,2,1,0:T(8,128)(2,1)}, f32[16,128]{1,0:T(8,128)}) custom-call(s32[8192]{0:T(1024)} %tok_ref.1, f32[1]{0:T(128)} %bitcast.1.rtau_ref, bf16[256,2048]{1,0:T(8,128)(2,1)} %q_ref.3, bf16[8192,2048]{1,0:T(8,128)(2,1)} %k_ref.1), custom_call_target="tpu_custom_call" | custom-call | tf_op jit(solution)/shard_map/local_histogram/pallas_call | solution.py:450
  47.8 0.0 copy-start
  47.8 0.7 copy-done
  48.5 57.8 %group_exchange.1 = f32[64,4000]{1,0:T(8,128)S(1)} custom-call(f32[1]{0:T(128)} %bitcast.3.lam_ref, f32[16,128]{1,0:T(8,128)S(1)} %copy-done, bf16[256,2048]{1,0:T(8,128)(2,1)} %q_ref.3, bf16[4,2,4,2048,128]{4,3,2,1,0:T(8,128)(2,1)} %get-tuple-element.8.h_ref, bf16[4000,2048]{1,0:T(8,128)(2,1)} %bitcast.4), custom_call_target="tpu_custom_call" | custom-call | tf_op jit(solution)/shard_map/group_exchange/pallas_call | solution.py:477
  106.3 1.0 copy.10
Async XLA Ops:
  47.8 0.7 copy-start

commit v5 on v4

--- a/solution.py
+++ b/solution.py
@@ -17,11 +17,11 @@
 ORDER = ((0, 0), (0, 1), (0, 2), (1, 0), (0, 3), (1, 1), (2, 0), (1, 2), (2, 1), (3, 0), (1, 3), (2, 2), (3, 1), (2, 3), (3, 2), (3, 3))
 
 
-def _scores_kernel(n_blocks, owners, vocab_loc, tok_ref, rtau_ref, q_ref, k_ref, h_ref, stat_ref, hist, vals, top, stage, flag_v, flag_s, word_v, word_s, sem, token_sem):
+def _scores_kernel(n_blocks, owners, vocab_loc, tok_ref, rtau_ref, q_ref, k_hbm, h_ref, stat_ref, kbuf, hist, vals, top, stage, flag_v, flag_s, word_v, word_s, sem, token_sem, k_sem):
     step = pl.program_id(0)
     n_core = h_ref.shape[1]
     first_half = h_ref.shape[3]
-    block = k_ref.shape[0]
+    slots, block, _ = kbuf.shape
     rows = q_ref.shape[0]
     keys = vals.shape[0] // 2
     filled = 2 * vocab_loc * owners
@@ -32,8 +32,14 @@
     zero_rows = filled // n_blocks
     hist[pl.ds(pl.multiple_of(step * zero_rows, 8), zero_rows), :] = jnp.zeros((zero_rows, LANES), F32)
 
+    def key_copy(n):
+        slot = lax.rem(n, slots)
+        return pltpu.make_async_copy(k_hbm.at[pl.ds(pl.multiple_of(n * block, block), block), :], kbuf.at[slot], k_sem.at[slot])
+
     @pl.when(step == 0)
     def _():
+        for n in range(min(slots - 1, n_blocks)):
+            key_copy(n).start()
         top[...] = jnp.full(top.shape, -jnp.inf, F32)
         rest = hist.shape[0] - filled
         hist[filled:, :] = jnp.zeros((rest, LANES), F32)
@@ -48,6 +54,12 @@
         for copy in token_copies:
             copy.start()
 
+    @pl.when(step + slots - 1 < n_blocks)
+    def _():
+        key_copy(step + slots - 1).start()
+
+    key_copy(step).wait()
+    k_ref = kbuf.at[lax.rem(step, slots)]
     sub = min(256, block)
     for part in range(block // sub):
         key = k_ref[part * sub : (part + 1) * sub, :]
@@ -291,27 +303,29 @@
 
     ring1_copies, ring2_copies = {}, {}
 
-    def process(st, k, i):
+    def process(st, k, i, h=None):
+        lo, count = (0, size) if h is None else (h * (size // 2), size // 2)
         slot = st * ring + k
         sub = sub_of(st, i)
         band = block_of(st, k) if st < 2 else sub
-        if k == 0 or i == 0:
-            sem = i if k == 0 else ring + k - 1
-            own_copies[st, sem].wait()
-            par_copies[st, sem].wait_recv()
-        if k > 0:
-            ring1_copies[st, k - 1, i].wait_recv()
         last = k == ring - 1
-        if last and i > 0:
-            ring2_copies[st, i - 1].wait_recv()
+        if not h:
+            if k == 0 or i == 0:
+                sem = i if k == 0 else ring + k - 1
+                own_copies[st, sem].wait()
+                par_copies[st, sem].wait_recv()
+            if k > 0:
+                ring1_copies[st, k - 1, i].wait_recv()
+        if last and i > 0 and (st, i - 1, h or 0) in ring2_copies:
+            ring2_copies[st, i - 1, h or 0].wait_recv()
         f_own = jnp.concatenate([fs[0 if k == 0 else 2, band]] * 2, axis=0)
         f_par = jnp.concatenate([fs[1 if k == 0 else 3, band]] * 2, axis=0)
         f_ring = jnp.concatenate([fs[5 + st, band]] * 2, axis=0) if k == 1 else None
-        unroll = 8 if size % 128 == 0 else 1
+        unroll = 8 if count % 128 == 0 else 1
 
         def body(t, _):
             for u in range(unroll):
-                here = pl.ds(pl.multiple_of(t * (16 * unroll) + 16 * u, 16), 16)
+                here = pl.ds(pl.multiple_of(lo + t * (16 * unroll) + 16 * u, 16), 16)
                 value = own[slot, sub, here, :].astype(F32) * f_own + par[slot, sub, here, :].astype(F32) * f_par
                 if k > 0:
                     came = ring1[st, k - 1, i, here, :].astype(F32)
@@ -324,16 +338,18 @@
                     own[slot, sub, here, :] = value.astype(BF16)
             return 0
 
-        lax.fori_loop(0, size // (16 * unroll), body, 0)
+        lax.fori_loop(0, count // (16 * unroll), body, 0)
         d = direction(st)
         if not last:
             peer = along_y(d) if st < 2 else along_x(d)
             ring1_copies[st, k, i] = remote(own.at[slot, sub], ring1.at[st, k, i], r1_send.at[st, k, i], r1_recv.at[st, k, i], peer)
         elif i < ring - 1:
             peer = along_x(d) if st < 2 else along_y(d)
-            ring2_copies[st, i] = remote(own.at[slot, sub], ring2.at[st, i], r2_send.at[st, i], r2_recv.at[st, i], peer)
+            rows = pl.ds(lo, count)
+            half = h or 0
+            ring2_copies[st, i, half] = remote(own.at[slot, sub, rows, :], ring2.at[st, i, rows, :], r2_send.at[st, i, half], r2_recv.at[st, i, half], peer)
         else:
-            finish(st)
+            finish(st, lo, count)
 
     def head(q):
         if q == 0:
@@ -385,11 +401,11 @@
             copy.wait_recv()
             lm["now"] = merge(lm["now"], load(lm_recv.at[n]))
 
-    def finish(st):
+    def finish(st, lo, rows):
         scale = lam / fs[4, s]
         lm_scale = lm["scale"]
-        wide = min(LANES, size)
-        for b in range(size // wide):
+        wide = min(LANES, rows)
+        for b in range(lo // wide, (lo + rows) // wide):
             at = st * size + b * wide
             p_knn = fin[b * wide : (b + 1) * wide, :].reshape(wide // 8, 8, LANES) * scale[None]
             p_lm = logit[at : at + wide, :].reshape(wide // 8, 8, LANES) * lm_scale[None]
@@ -400,8 +416,9 @@
                 out_ref[:, first_half + at : first_half + at + count] = mixed[64:128, :count]
 
     for place, (k, i) in enumerate(ORDER):
-        for st in range(4):
-            process(st, k, i)
+        for h in (0, 1) if k == ring - 1 and i > 0 else (None,):
+            for st in range(4):
+                process(st, k, i, h)
         if place == 0:
             knn_collect()
             knn_publish(1, [(ring - 1 + d, along_x(d)) for d in range(1, ring)])
@@ -436,7 +453,7 @@
         keys = store_keys.shape[0]
         first_half = -(-vocab_loc // (2 * 4 * LANES)) * 4 * LANES
         size = first_half // 4
-        block = min(1024, keys)
+        block = min(512, keys)
         n_blocks = keys // block
         n_batches = keys // BATCH
         hist_rows = 2 * ((model_devs - 1) * vocab_loc + 2 * first_half)
@@ -455,10 +472,11 @@
                 pl.BlockSpec((keys,), lambda i: (0,)),
                 smem,
                 pl.BlockSpec((rows, hidden), lambda i: (0, 0)),
-                pl.BlockSpec((block, hidden), lambda i: (i, 0)),
+                hbm,
             ],
             out_specs=(any_space, pl.BlockSpec((16, LANES), lambda i: (0, 0))),
             scratch_shapes=[
+                pltpu.VMEM((4, block, hidden), BF16),
                 pltpu.VMEM((hist_rows, LANES), F32),
                 pltpu.VMEM((2 * keys, LANES), F32),
                 pltpu.VMEM((8, rows), F32),
@@ -469,6 +487,7 @@
                 pltpu.SMEM((1, keys // 2), jnp.int32),
                 dma((2,)),
                 dma((2,)),
+                dma((4,)),
             ],
             compiler_params=pltpu.CompilerParams(vmem_limit_bytes=62 * 1024 * 1024),
             name="local_histogram",
@@ -497,7 +516,7 @@
                 pltpu.VMEM((2, 16, LANES), F32),
                 dma((4, 2 * ring - 1)), dma((4, 2 * ring - 1)), dma((4, 2 * ring - 1)),
                 dma((4, ring - 1, ring)), dma((4, ring - 1, ring)),
-                dma((4, ring - 1)), dma((4, ring - 1)),
+                dma((4, ring - 1, 2)), dma((4, ring - 1, 2)),
                 dma((2 * ring + 1,)), dma((2 * ring + 1,)),
                 dma((ring,)), dma((ring,)),
                 dma((2, 4)),

time: 108 us -> 107 us (level)
  no operation moved by 1% of the time
where the time goes in v5:
time: 107 us
  Pallas kernels  104 us (97%)
  local copies, waits for them, and re-layouts  1.66 us (2%)
  between operations  1.36 us (1%)
    pallas_call x1, Pallas kernels, local_step(): pl.pallas_call(functools.partial(_exchange_kernel, ring, vocab_loc), out_...  57.2 us
    pallas_call x1, Pallas kernels, local_step(): pl.pallas_call(functools.partial(_scores_kernel, n_blocks, model_devs, vo...  46.3 us

profile of v5, /device:TPU:97, one launch (start us, length us, event | category | flops | bytes accessed | tf_op | source)
XLA Modules:
  0.0 106.6 jit_solution(5948492019596158247)
XLA Ops:
  1.3 46.3 %local_histogram.1 = (bf16[4,2,4,2048,128]{4,3,2,1,0:T(8,128)(2,1)}, f32[16,128]{1,0:T(8,128)}) custom-call(s32[8192]{0:T(1024)} %tok_ref.1, f32[1]{0:T(128)} %bitcast.1.rtau_ref, bf16[256,2048]{1,0:T(8,128)(2,1)} %q_ref.3, bf16[8192,2048]{1,0:T(8,128)(2,1)} %k_hbm.1), custom_call_target="tpu_custom_call" | custom-call | tf_op jit(solution)/shard_map/local_histogram/pallas_call | solution.py:467
  47.7 0.0 copy-start
  47.7 0.7 copy-done
  48.4 57.2 %group_exchange.1 = f32[64,4000]{1,0:T(8,128)S(1)} custom-call(f32[1]{0:T(128)} %bitcast.3.lam_ref, f32[16,128]{1,0:T(8,128)S(1)} %copy-done, bf16[256,2048]{1,0:T(8,128)(2,1)} %q_ref.3, bf16[4,2,4,2048,128]{4,3,2,1,0:T(8,128)(2,1)} %get-tuple-element.8.h_ref, bf16[4000,2048]{1,0:T(8,128)(2,1)} %bitcast.4), custom_call_target="tpu_custom_call" | custom-call | tf_op jit(solution)/shard_map/group_exchange/pallas_call | solution.py:496
  105.6 1.0 copy.10
Async XLA Ops:
  47.7 0.7 copy-start

commit v6 on v5

--- a/solution.py
+++ b/solution.py
@@ -12,6 +12,7 @@
 LANES = 128
 BATCH = 32
 GROUP = 16
+SUB = 256
 PACK_TILES = 32
 MESH_ID = pl.DeviceIdType.MESH
 ORDER = ((0, 0), (0, 1), (0, 2), (1, 0), (0, 3), (1, 1), (2, 0), (1, 2), (2, 1), (3, 0), (1, 3), (2, 2), (3, 1), (2, 3), (3, 2), (3, 3))
@@ -30,7 +31,6 @@
     token_copies = [pltpu.make_async_copy(word_v, word_s, token_sem.at[0]), pltpu.make_async_copy(flag_v, flag_s, token_sem.at[1])]
 
     zero_rows = filled // n_blocks
-    hist[pl.ds(pl.multiple_of(step * zero_rows, 8), zero_rows), :] = jnp.zeros((zero_rows, LANES), F32)
 
     def key_copy(n):
         slot = lax.rem(n, slots)
@@ -60,7 +60,8 @@
 
     key_copy(step).wait()
     k_ref = kbuf.at[lax.rem(step, slots)]
-    sub = min(256, block)
+    hist[pl.ds(pl.multiple_of(step * zero_rows, 8), zero_rows), :] = jnp.zeros((zero_rows, LANES), F32)
+    sub = min(SUB, block)
     for part in range(block // sub):
         key = k_ref[part * sub : (part + 1) * sub, :]
         dots = lax.dot_general(key, q_ref[...], (((1,), (1,)), ((), ())), preferred_element_type=F32)
@@ -453,7 +454,7 @@
         keys = store_keys.shape[0]
         first_half = -(-vocab_loc // (2 * 4 * LANES)) * 4 * LANES
         size = first_half // 4
-        block = min(512, keys)
+        block = min(1024, keys)
         n_blocks = keys // block
         n_batches = keys // BATCH
         hist_rows = 2 * ((model_devs - 1) * vocab_loc + 2 * first_half)
@@ -476,7 +477,7 @@
             ],
             out_specs=(any_space, pl.BlockSpec((16, LANES), lambda i: (0, 0))),
             scratch_shapes=[
-                pltpu.VMEM((4, block, hidden), BF16),
+                pltpu.VMEM((3, block, hidden), BF16),
                 pltpu.VMEM((hist_rows, LANES), F32),
                 pltpu.VMEM((2 * keys, LANES), F32),
                 pltpu.VMEM((8, rows), F32),
@@ -487,7 +488,7 @@
                 pltpu.SMEM((1, keys // 2), jnp.int32),
                 dma((2,)),
                 dma((2,)),
-                dma((4,)),
+                dma((3,)),
             ],
             compiler_params=pltpu.CompilerParams(vmem_limit_bytes=62 * 1024 * 1024),
             name="local_histogram",

time: 107 us -> 106 us (level)
  no operation moved by 1% of the time
where the time goes in v6:
time: 106 us
  Pallas kernels  103 us (97%)
  local copies, waits for them, and re-layouts  1.66 us (2%)
  between operations  1.36 us (1%)
    pallas_call x1, Pallas kernels, local_step(): pl.pallas_call(functools.partial(_exchange_kernel, ring, vocab_loc), out_...  57.2 us
    pallas_call x1, Pallas kernels, local_step(): pl.pallas_call(functools.partial(_scores_kernel, n_blocks, model_devs, vo...  45.8 us

profile of v6, /device:TPU:97, one launch (start us, length us, event | category | flops | bytes accessed | tf_op | source)
XLA Modules:
  0.0 106.0 jit_solution(6336019203765872012)
XLA Ops:
  1.3 45.8 %local_histogram.1 = (bf16[4,2,4,2048,128]{4,3,2,1,0:T(8,128)(2,1)}, f32[16,128]{1,0:T(8,128)}) custom-call(s32[8192]{0:T(1024)} %tok_ref.1, f32[1]{0:T(128)} %bitcast.1.rtau_ref, bf16[256,2048]{1,0:T(8,128)(2,1)} %q_ref.3, bf16[8192,2048]{1,0:T(8,128)(2,1)} %k_hbm.1), custom_call_target="tpu_custom_call" | custom-call | tf_op jit(solution)/shard_map/local_histogram/pallas_call | solution.py:468
  47.1 0.0 copy-start
  47.1 0.7 copy-done
  47.8 57.2 %group_exchange.1 = f32[64,4000]{1,0:T(8,128)S(1)} custom-call(f32[1]{0:T(128)} %bitcast.3.lam_ref, f32[16,128]{1,0:T(8,128)S(1)} %copy-done, bf16[256,2048]{1,0:T(8,128)(2,1)} %q_ref.3, bf16[4,2,4,2048,128]{4,3,2,1,0:T(8,128)(2,1)} %get-tuple-element.8.h_ref, bf16[4000,2048]{1,0:T(8,128)(2,1)} %bitcast.4), custom_call_target="tpu_custom_call" | custom-call | tf_op jit(solution)/shard_map/group_exchange/pallas_call | solution.py:497
  105.1 1.0 copy.10
Async XLA Ops:
  47.1 0.7 copy-start
